TPU v7x, 512 devices: a whole 4x8x8 slice. The times are simulated.
512 devices in a mesh: seq: 64 (over y_hi, x, z), bat: 8 (over y_lo, core).
Axes of the slice: x: 4, y: 8 (y_hi: 2, y_lo: 4; y = y_hi * 4 + y_lo), z: 8, core: 2. Of those that a mesh axis runs over, the one named last changes fastest.
Arguments:
- tokens: bfloat16 [8, 65536, 256], P('bat', 'seq'), may hold values from -6 to 6
- filter_spectrum: bfloat16 [2, 256, 256, 256], P(None, 'seq', None, 'bat'), may hold values from -6 to 6
- skip_gain: float32 [256], replicated, may hold values from 0.5 to 1.5
Outputs:
- mixed: bfloat16 [8, 65536, 256], P('bat', 'seq')
All inputs are finite; a program needn't handle non-finite values.
Results may differ from a plain program's by a relative error of at most 0.012.
Values may be sent and summed in bfloat16 or wider, within the bound.
No kernel may reach another device: no remote copies, remote signals or barrier semaphores. Data moves between devices by JAX's collectives and lax.ppermute only.
A program may use at most 64 MiB of HBM per device.

v0:
```python
import math

import jax
import jax.numpy as jnp
from jax import lax
from jax.sharding import PartitionSpec as P

N1 = 256
N2 = 256


def from_everyone(array, axis):
    copies = jnp.broadcast_to(array, (lax.axis_size(axis), *array.shape))
    return lax.all_to_all(copies, axis, split_axis=0, concat_axis=0, tiled=True)


def joined_along(pieces, dim):
    pieces = jnp.moveaxis(pieces, 0, dim)
    dims = pieces.shape
    return pieces.reshape(*dims[:dim], dims[dim] * dims[dim + 1], *dims[dim + 2 :])


def gather_directly(array, axis, dim):
    pieces = from_everyone(array, axis)
    return joined_along(pieces, dim)


def cos_sin(points):
    steps_range = jnp.arange(points, dtype=jnp.int32)
    index_grid = steps_range[:, None] * steps_range[None, :] % points
    phase_angle = index_grid.astype(jnp.float32) * (2.0 * math.pi / points)
    return (jnp.cos(phase_angle), jnp.sin(phase_angle))


def real_table(points):
    cosine, sine_vals = cos_sin(points)
    return jnp.stack([cosine, -sine_vals], axis=1).astype(jnp.bfloat16)


def complex_table(points, signum, factor):
    cosine, sine_vals = cos_sin(points)
    top_rows = jnp.stack([cosine, signum * sine_vals], axis=1)
    low_rows = jnp.stack([-signum * sine_vals, cosine], axis=1)
    return (jnp.stack([top_rows, low_rows], axis=0) * factor).astype(jnp.bfloat16)


def final_table(points):
    cosine, sine_vals = cos_sin(points)
    return (jnp.stack([cosine, -sine_vals], axis=0) / points).astype(jnp.bfloat16)


def twiddle_phase(first_rows, second_rows, period):
    index_grid = first_rows[:, None] * second_rows[None, :] % period
    phase_angle = index_grid.astype(jnp.float32) * (2.0 * math.pi / period)
    return (jnp.cos(phase_angle)[..., None], jnp.sin(phase_angle)[..., None])


def multiply(values, filters):
    chosen = values.astype(jnp.float32)
    weights = gather_directly(filters, "bat", 3).astype(jnp.float32)[:, None]
    real_part = chosen[0] * weights[0] - chosen[1] * weights[1]
    imag_part = chosen[0] * weights[1] + chosen[1] * weights[0]
    return jnp.stack([real_part, imag_part]).astype(jnp.bfloat16)


def body(tokens, filter_spectrum, skip_gain):
    seq_count = lax.axis_size("seq")
    device_index = lax.axis_index("seq")
    batch_rows, local_length, channels = tokens.shape
    rows_local = N1 // seq_count
    cols_local = N2 // seq_count
    period = N1 * N2
    laid_out = tokens.reshape(batch_rows, rows_local, N2, channels)
    columns = lax.all_to_all(laid_out, "seq", split_axis=2, concat_axis=1, tiled=True)
    first_section = jnp.einsum(
        "bnmc,nsk->sbkmc", columns, real_table(N1), preferred_element_type=jnp.float32
    )
    own_cols = device_index * cols_local + jnp.arange(cols_local, dtype=jnp.int32)
    cos_tw, sin_tw = twiddle_phase(jnp.arange(N1, dtype=jnp.int32), own_cols, period)
    real_part = first_section[0] * cos_tw + first_section[1] * sin_tw
    imag_part = first_section[1] * cos_tw - first_section[0] * sin_tw
    turned = jnp.stack([real_part, imag_part]).astype(jnp.bfloat16)
    rows_block = lax.all_to_all(turned, "seq", split_axis=2, concat_axis=3, tiled=True)
    spectrum = jnp.einsum(
        "rbknc,rnsj->sbkjc",
        rows_block,
        complex_table(N2, -1.0, 1.0),
        preferred_element_type=jnp.float32,
    ).astype(jnp.bfloat16)
    product = multiply(spectrum, filter_spectrum)
    back_section = jnp.einsum(
        "rbkjc,rjsn->sbknc",
        product,
        complex_table(N2, 1.0, 1.0 / N2),
        preferred_element_type=jnp.float32,
    )
    own_rows = device_index * rows_local + jnp.arange(rows_local, dtype=jnp.int32)
    cos_back, sin_back = twiddle_phase(own_rows, jnp.arange(N2, dtype=jnp.int32), period)
    real_back = back_section[0] * cos_back - back_section[1] * sin_back
    imag_back = back_section[0] * sin_back + back_section[1] * cos_back
    turned_back = jnp.stack([real_back, imag_back]).astype(jnp.bfloat16)
    mixed_cols = lax.all_to_all(turned_back, "seq", split_axis=3, concat_axis=2, tiled=True)
    filtered = jnp.einsum(
        "rbknc,rkm->bmnc", mixed_cols, final_table(N1), preferred_element_type=jnp.float32
    )
    result = (filtered + skip_gain * columns.astype(jnp.float32)).astype(jnp.bfloat16)
    restored = lax.all_to_all(result, "seq", split_axis=1, concat_axis=2, tiled=True)
    return restored.reshape(batch_rows, local_length, channels)


def solution(mesh):
    placed = (P("bat", "seq", None), P(None, "seq", None, "bat"), P())
    return jax.shard_map(
        body, mesh=mesh, in_specs=placed, out_specs=P("bat", "seq", None), check_vma=False
    )
```

profile of v0, /device:TPU:1, one launch (start us, length us, event | category | flops | bytes accessed | tf_op | source)
XLA Modules:
  0.0 189.9 jit_solution(17914769664170347526)
XLA Ops:
  0.0 1.5 copy.41
  1.5 36.1 %all_to_all.65 = bf16[1,4,256,256]{3,1,0,2:T(4,128)(2,1)S(1)} all-to-all(bf16[1,4,256,256]{3,1,0,2:T(4,128)(2,1)S(1)} %copy.41), channel_id=1, replica_groups=mesh['seq'=64,'bat'=8] {'seq'}, dimensions={2} | all-to-all | bytes 1048576 | tf_op jit(solution)/shard_map/all_to_all | solution.py:74
  37.6 1.1 broadcast_in_dim.2
  38.7 9.5 %all-to-all-start.2 = ((bf16[8,2,4,256,32]{3,4,2,1,0:T(8,128)(2,1)}), bf16[8,2,4,256,32]{3,4,2,1,0:T(8,128)(2,1)S(1)}, u32[]{:S(2)}, u32[]{:S(2)}) async-start(bf16[8,2,4,256,32]{3,4,2,1,0:T(8,128)(2,1)} %broadcast_in_dim.2), calls=%async_computation.2 | async-start | bytes 2097152 | tf_op jit(solution)/shard_map/all_to_all | solution.py:14
  48.2 1.1 negate_convert_fusion
  49.8 0.4 fusion.15
  50.2 0.3 fusion.7
  50.7 1.8 copy.43
  52.5 21.4 %all-to-all-done.2 = bf16[8,2,4,256,32]{3,4,2,1,0:T(8,128)(2,1)S(1)} async-done(((bf16[8,2,4,256,32]{3,4,2,1,0:T(8,128)(2,1)}), bf16[8,2,4,256,32]{3,4,2,1,0:T(8,128)(2,1)S(1)}, u32[]{:S(2)}, u32[]{:S(2)}) %all-to-all-start.2) | async-done | bytes 1048608 | tf_op jit(solution)/shard_map/all_to_all | solution.py:14
  73.8 6.0 %all-to-all-start.1 = ((bf16[2,1,256,4,256]{4,3,1,0,2:T(4,128)(2,1)}), bf16[2,1,256,4,256]{4,3,1,0,2:T(4,128)(2,1)}, u32[]{:S(2)}, u32[]{:S(2)}) async-start(bf16[2,1,256,4,256]{4,3,1,0,2:T(4,128)(2,1)} %copy.43), calls=%async_computation.1 | async-start | bytes 2097152 | tf_op jit(solution)/shard_map/all_to_all | solution.py:83
  79.8 1.0 fusion.35
  80.8 1.0 fusion.34
  81.8 1.0 broadcast_multiply_fusion
  82.8 1.1 maximum_bitcast_fusion
  84.3 1.1 fusion.52
  85.7 1.6 copy.48
  87.3 21.5 %all-to-all-done.1 = bf16[2,1,256,4,256]{4,3,1,0,2:T(4,128)(2,1)} async-done(((bf16[2,1,256,4,256]{4,3,1,0,2:T(4,128)(2,1)}), bf16[2,1,256,4,256]{4,3,1,0,2:T(4,128)(2,1)}, u32[]{:S(2)}, u32[]{:S(2)}) %all-to-all-start.1) | async-done | bytes 1048608 | tf_op jit(solution)/shard_map/all_to_all | solution.py:83
  108.8 2.6 %copy.82 = bf16[2,1,64,4,4,256]{5,4,2,0,3,1:T(4,128)(2,1)} copy(bf16[2,1,64,4,4,256]{5,4,0,3,2,1:T(4,128)(2,1)} %bitcast.14) | data formatting | bytes 2097152 | tf_op jit(solution)/shard_map/all_to_all | solution.py:83
  111.4 2.2 %reshape.436 = bf16[2,4,256,256,1]{3,2,0,1,4:T(8,128)(2,1)} reshape(bf16[2,1,4,64,4,256]{5,4,3,0,2,1:T(4,128)(2,1)} %bitcast.108) | data formatting | bytes 2097152 | tf_op jit(solution)/shard_map/reshape.15
  113.6 1.9 %convert_bitcast_fusion.1 = (f32[2,1,4,256,256]{4,3,2,0,1:T(8,128)S(1)}, f32[2,1,4,256,256]{4,3,2,1,0:T(8,128)S(1)}) fusion(bf16[2,4,256,256,1]{3,2,0,1,4:T(8,128)(2,1)} %reshape.436, bf16[1,256,2,256]{1,3,2,0:T(8,128)(2,1)S(1)} %get-tuple-element.18, bf16[1,256,2,256]{1,3,2,0:T(8,128)(2,1)S(1)} %get-tuple-element.17), kind=kOutput, calls=%fused_computation.1 | convolution fusion | flops 538181632 | bytes 5767168 | tf_op jit(solution)/shard_map/rbknc,rnsj->sbkjc/dot_general | solution.py:84
  115.5 0.5 subtract_convert_fusion.1
  116.0 0.5 copy-done
  116.7 0.7 convolution_bitcast_fusion
  117.9 1.8 copy.54
  119.7 8.8 %all-to-all-start.3 = ((bf16[2,1,4,256,256]{4,2,0,1,3:T(4,128)(2,1)}), bf16[2,1,4,256,256]{4,2,0,1,3:T(4,128)(2,1)S(1)}, u32[]{:S(2)}, u32[]{:S(2)}) async-start(bf16[2,1,4,256,256]{4,2,0,1,3:T(4,128)(2,1)} %copy.54), calls=%async_computation.3 | async-start | bytes 2097152 | tf_op jit(solution)/shard_map/all_to_all | solution.py:102
  128.5 1.7 sine_negate_fusion
  130.3 22.1 %all-to-all-done.3 = bf16[2,1,4,256,256]{4,2,0,1,3:T(4,128)(2,1)S(1)} async-done(((bf16[2,1,4,256,256]{4,2,0,1,3:T(4,128)(2,1)}), bf16[2,1,4,256,256]{4,2,0,1,3:T(4,128)(2,1)S(1)}, u32[]{:S(2)}, u32[]{:S(2)}) %all-to-all-start.3) | async-done | bytes 1048608 | tf_op jit(solution)/shard_map/all_to_all | solution.py:102
  152.5 0.4 copy.81
  153.2 1.4 fusion.3
  154.5 0.4 copy.56
  155.0 33.8 %all_to_all.66 = bf16[1,256,4,256]{3,2,0,1:T(4,128)(2,1)S(1)} all-to-all(bf16[1,256,4,256]{3,2,0,1:T(4,128)(2,1)S(1)} %copy.56), channel_id=1, replica_groups=mesh['seq'=64,'bat'=8] {'seq'}, dimensions={1} | all-to-all | bytes 1048576 | tf_op jit(solution)/shard_map/all_to_all | solution.py:107
  189.0 0.9 reshape.431
  (21 shorter events, 2.5 us)
Async XLA Ops:
  0.0 37.6 %copy-start.2 = (bf16[2,4,256,32]{2,3,1,0:T(8,128)(2,1)S(1)}, bf16[2,4,256,32]{2,3,1,0:T(8,128)(2,1)}, u32[]{:S(2)}) copy-start(bf16[2,4,256,32]{2,3,1,0:T(8,128)(2,1)} %param.4) | copy-start | bytes 393220
  38.7 35.1 %all-to-all-start.2 = ((bf16[8,2,4,256,32]{3,4,2,1,0:T(8,128)(2,1)}), bf16[8,2,4,256,32]{3,4,2,1,0:T(8,128)(2,1)S(1)}, u32[]{:S(2)}, u32[]{:S(2)}) async-start(bf16[8,2,4,256,32]{3,4,2,1,0:T(8,128)(2,1)} %broadcast_in_dim.2), calls=%async_computation.2 | async-start | bytes 2097152 | tf_op jit(solution)/shard_map/all_to_all | solution.py:14
  73.8 35.0 %all-to-all-start.1 = ((bf16[2,1,256,4,256]{4,3,1,0,2:T(4,128)(2,1)}), bf16[2,1,256,4,256]{4,3,1,0,2:T(4,128)(2,1)}, u32[]{:S(2)}, u32[]{:S(2)}) async-start(bf16[2,1,256,4,256]{4,3,1,0,2:T(4,128)(2,1)} %copy.43), calls=%async_computation.1 | async-start | bytes 2097152 | tf_op jit(solution)/shard_map/all_to_all | solution.py:83
  115.5 1.0 copy-start
  115.5 1.2 copy-start.1
  119.7 32.8 %all-to-all-start.3 = ((bf16[2,1,4,256,256]{4,2,0,1,3:T(4,128)(2,1)}), bf16[2,1,4,256,256]{4,2,0,1,3:T(4,128)(2,1)S(1)}, u32[]{:S(2)}, u32[]{:S(2)}) async-start(bf16[2,1,4,256,256]{4,2,0,1,3:T(4,128)(2,1)} %copy.54), calls=%async_computation.3 | async-start | bytes 2097152 | tf_op jit(solution)/shard_map/all_to_all | solution.py:102
  152.5 0.7 copy-start.3
where the time goes:
time: 191 us; the launch traced here: 190 us
  blocking collectives  69.9 us (37%)
  waiting for transfers between devices  65 us (34%)
  starting transfers between devices  24.2 us (13%)
  local copies, waits for them, and re-layouts  17.2 us (9%)
  other arithmetic  8.78 us (5%)
  matrix products  4.47 us (2%)
    all_to_all x1, blocking collectives, body(): lax.all_to_all(laid_out, 'seq', split_axis=2, concat_axis=1, tiled=True)  36.1 us
    all_to_all x1, blocking collectives, body(): lax.all_to_all(result, 'seq', split_axis=1, concat_axis=2, tiled=True)  33.8 us
    all_to_all x1, waiting for transfers between devices, body(): lax.all_to_all(turned_back, 'seq', split_axis=3, concat_axis=2, tiled=True)  22.1 us
    all_to_all x1, waiting for transfers between devices, body(): lax.all_to_all(turned, 'seq', split_axis=2, concat_axis=3, tiled=True)  21.5 us
    all_to_all x1, waiting for transfers between devices, from_everyone(): return lax.all_to_all(copies, axis, split_axis=0, concat_axis=0, tiled=True)  21.4 us
    all_to_all x1, starting transfers between devices, from_everyone(): return lax.all_to_all(copies, axis, split_axis=0, concat_axis=0, tiled=True)  9.5 us
    all_to_all x1, starting transfers between devices, body(): lax.all_to_all(turned_back, 'seq', split_axis=3, concat_axis=2, tiled=True)  8.78 us
    all_to_all x1, starting transfers between devices, body(): lax.all_to_all(turned, 'seq', split_axis=2, concat_axis=3, tiled=True)  5.96 us
  transfers between devices with their start and end apart: 3, of which 3 were waited for; matrix products, arithmetic and copies ran while one was open for 7% of the time, Pallas kernels for 0%

commit v1 on v0

v1 whole, which is shorter than its diff:
```python
import math

import jax
import jax.numpy as jnp
from jax import lax
from jax.experimental import pallas as pl
from jax.experimental.pallas import tpu as pltpu
from jax.sharding import Mesh
from jax.sharding import PartitionSpec as P

N1 = 256
N2 = 256
HALF = 128


def cos_sin(points):
    steps_range = jnp.arange(points, dtype=jnp.int32)
    index_grid = steps_range[:, None] * steps_range[None, :] % points
    phase_angle = index_grid.astype(jnp.float32) * (2.0 * math.pi / points)
    return (jnp.cos(phase_angle), jnp.sin(phase_angle))


def twiddle_phase():
    period = N1 * N2
    index_grid = jnp.arange(N1, dtype=jnp.int32)[:, None] * jnp.arange(N2, dtype=jnp.int32)[None, :] % period
    phase_angle = index_grid.astype(jnp.float32) * (2.0 * math.pi / period)
    return (jnp.cos(phase_angle), jnp.sin(phase_angle))


def spread_rows(table):
    eye = jnp.eye(2, dtype=table.dtype)
    wide = eye[:, None, None, :] * table[None, :, :, None]
    return wide.reshape(2 * N1, 2 * N1)


def tables():
    cosine, sine = cos_sin(N1)
    c16, s16 = cosine.astype(jnp.bfloat16), sine.astype(jnp.bfloat16)
    ci = (cosine / N1).astype(jnp.bfloat16)
    si = (sine / N1).astype(jnp.bfloat16)
    first = jnp.concatenate([spread_rows(c16), spread_rows(-s16)], axis=0)
    second = jnp.concatenate(
        [jnp.concatenate([c16, -s16], axis=1), jnp.concatenate([s16, c16], axis=1)], axis=0
    )
    third = jnp.concatenate(
        [jnp.concatenate([ci, si], axis=1), jnp.concatenate([-si, ci], axis=1)], axis=0
    )
    fourth = jnp.concatenate([spread_rows(ci).T, spread_rows(-si).T], axis=1)
    return first, second, third, fourth


def row_order():
    want = jnp.arange(2 * N1, dtype=jnp.int32)
    part, k1 = want // N1, want % N1
    source = (k1 // 4) * 8 + part * 4 + k1 % 4
    return (source[:, None] == jnp.arange(2 * N1, dtype=jnp.int32)[None, :]).astype(jnp.bfloat16)


def dot(a, b):
    return jnp.dot(a, b, preferred_element_type=jnp.float32)


def convolve(gain, u, filt, order, first, second, third, fourth, cos_tw, sin_tw, out):
    weights = dot(order[...], filt[...])
    wr, wi = weights[:N1], weights[N1:]
    c, s = cos_tw[...], sin_tw[...]
    batches = u.shape[0]
    section = dot(first[...], jnp.concatenate([u[b] for b in range(batches)], axis=1))
    for b in range(batches):
        lanes = slice(b * HALF, (b + 1) * HALF)
        piece = section[:, lanes]
        re = jnp.concatenate([piece[:N1], piece[N1 : 2 * N1]], axis=1)
        im = jnp.concatenate([piece[2 * N1 : 3 * N1], piece[3 * N1 :]], axis=1)
        turned = jnp.concatenate([re * c + im * s, im * c - re * s], axis=1).astype(jnp.bfloat16)
        spectrum = dot(turned, second[...])
        sr, si = spectrum[:, :N2], spectrum[:, N2:]
        product = jnp.concatenate([sr * wr - si * wi, sr * wi + si * wr], axis=1).astype(jnp.bfloat16)
        back = dot(product, third[...])
        br, bi = back[:, :N2], back[:, N2:]
        tr = (br * c - bi * s).astype(jnp.bfloat16)
        ti = (br * s + bi * c).astype(jnp.bfloat16)
        rows = jnp.concatenate([tr[:, :HALF], tr[:, HALF:], ti[:, :HALF], ti[:, HALF:]], axis=0)
        filtered = dot(fourth[...], rows)
        out[b] = (filtered + gain[0] * u[b].astype(jnp.float32)).astype(jnp.bfloat16)


def body(tokens, filter_spectrum, skip_gain):
    channels = tokens.shape[-1]
    channel = lax.axis_index("ylo") * lax.axis_size("seq") + lax.axis_index("seq")
    laid_out = tokens.reshape(8, HALF, channels).transpose(2, 0, 1)
    u = lax.all_to_all(laid_out, ("ylo", "seq"), split_axis=0, concat_axis=0, tiled=True)
    u = u.reshape(4, 2 * N1, HALF)
    mine = filter_spectrum.transpose(3, 0, 1, 2)
    both = lax.all_gather(mine, "core", axis=0, tiled=True)
    both = both.reshape(both.shape[0], 8, N2)
    filt = lax.all_to_all(both, "seq", split_axis=0, concat_axis=0, tiled=True)
    filt = filt.reshape(2 * N1, N2)
    gain = lax.dynamic_slice(skip_gain, (channel,), (1,))
    first, second, third, fourth = tables()
    cos_tw, sin_tw = twiddle_phase()
    vmem = pl.BlockSpec(memory_space=pltpu.VMEM)
    mixed = pl.pallas_call(
        convolve,
        out_shape=jax.ShapeDtypeStruct((4, 2 * N1, HALF), jnp.bfloat16),
        in_specs=[pl.BlockSpec(memory_space=pltpu.SMEM)] + [vmem] * 9,
        out_specs=vmem,
    )(gain, u, filt, row_order(), first, second, third, fourth, cos_tw, sin_tw)
    mixed = mixed.reshape(4 * 64, 8, HALF)
    back = lax.all_to_all(mixed, ("ylo", "seq"), split_axis=0, concat_axis=0, tiled=True)
    return back.transpose(1, 2, 0).reshape(1, 8 * HALF, channels)


def solution(mesh):
    names = mesh.axis_names
    assert names == ("seq", "bat")
    split = Mesh(mesh.devices.reshape(64, 4, 2), ("seq", "ylo", "core"))
    bat = ("ylo", "core")
    placed = (P(bat, "seq", None), P(None, "seq", None, bat), P())
    return jax.shard_map(
        body, mesh=split, in_specs=placed, out_specs=P(bat, "seq", None), check_vma=False
    )
```

time: 191 us -> 107 us (0.56)
  waiting for transfers between devices: 65 us -> 14.7 us
  blocking collectives: 69.9 us -> 36.3 us
  local copies, waits for them, and re-layouts: 17.2 us -> 6.69 us
  Pallas kernels: 0 us -> 7.78 us
  other arithmetic: 8.78 us -> 14.9 us
  matrix products: 4.47 us -> 0 us
    all_to_all x3 -> x2, waiting for transfers between devices: 65 us -> 14.7 us  [the longest x1 7.36 us: body(): filt = lax.all_to_all(both, 'seq', split_axis=0, concat_axis=0, tiled=True)]
    all_to_all x2 -> x1, blocking collectives: 69.9 us -> 27.6 us  [body(): lax.all_to_all(mixed, ('ylo', 'seq'), split_axis=0, concat_axis=0, tiled=...]
    all_gather x0 -> x1, blocking collectives: none -> 8.67 us  [body(): both = lax.all_gather(mine, 'core', axis=0, tiled=True)]
    pallas_call x0 -> x1, Pallas kernels: none -> 7.78 us  [body(): pl.pallas_call(convolve, out_shape=jax.ShapeDtypeStruct((4, 2 * N1, HALF)...]
    another operation x4 -> x0, local copies, waits for them, and re-layouts: 6.05 us -> none
    concatenate x0 -> x4, other arithmetic: none -> 4.84 us  [the longest x1 1.8 us: tables(): jnp.concatenate([jnp.concatenate([c16, -s16], axis=1), jnp.concatenate([s...]
    another operation x9 -> x0, other arithmetic: 4.59 us -> none
    dot_general x4 -> x0, matrix products: 4.47 us -> none  [the longest x1 1.93 us: body(): jnp.einsum('rbknc,rnsj->sbkjc', rows_block, complex_table(N2, -1.0, 1.0),...]
  transfers between devices with their start and end apart: 3 -> 2, of which waited for: 3 -> 2; matrix products, arithmetic and copies ran while one was open for 7% -> 17% of each run, Pallas kernels for 0% -> 0%
where the time goes in v1:
time: 107 us; the launch traced here: 105 us
  blocking collectives  36.3 us (34%)
  starting transfers between devices  24.9 us (23%)
  other arithmetic  14.9 us (14%)
  waiting for transfers between devices  14.7 us (14%)
  Pallas kernels  7.78 us (7%)
  local copies, waits for them, and re-layouts  6.69 us (6%)
    all_to_all x1, blocking collectives, body(): lax.all_to_all(mixed, ('ylo', 'seq'), split_axis=0, concat_axis=0, tiled=...  27.6 us
    all_to_all x1, starting transfers between devices, body(): filt = lax.all_to_all(both, 'seq', split_axis=0, concat_axis=0, tiled=True)  13.4 us
    all_to_all x1, starting transfers between devices, body(): lax.all_to_all(laid_out, ('ylo', 'seq'), split_axis=0, concat_axis=0, til...  11.5 us
    all_gather x1, blocking collectives, body(): both = lax.all_gather(mine, 'core', axis=0, tiled=True)  8.67 us
    pallas_call x1, Pallas kernels, body(): pl.pallas_call(convolve, out_shape=jax.ShapeDtypeStruct((4, 2 * N1, HALF)...  7.78 us
    all_to_all x1, waiting for transfers between devices, body(): filt = lax.all_to_all(both, 'seq', split_axis=0, concat_axis=0, tiled=True)  7.36 us
    all_to_all x1, waiting for transfers between devices, body(): lax.all_to_all(laid_out, ('ylo', 'seq'), split_axis=0, concat_axis=0, til...  7.31 us
    unnamed x16, local copies, waits for them, and re-layouts  2.19 us
  transfers between devices with their start and end apart: 2, of which 2 were waited for; matrix products, arithmetic and copies ran while one was open for 17% of the time, Pallas kernels for 0%

profile of v1, /device:TPU:1, one launch (start us, length us, event | category | flops | bytes accessed | tf_op | source)
XLA Modules:
  0.0 105.4 jit_solution(11084024745705851260)
XLA Ops:
  0.0 8.7 %all_gather.3 = bf16[64,2,4,256]{3,0,2,1:T(8,128)(2,1)S(1)} all-gather(bf16[32,2,4,256]{3,0,2,1:T(8,128)(2,1)} %bitcast.47), channel_id=1, replica_groups=mesh['seq'=64,'ylo'=4,'core'=2] {'core'}, dimensions={0}, use_global_device_ids=true | all-gather | bytes 393216 | tf_op jit(solution)/shard_map/all_gather | solution.py:94
  8.7 0.8 copy.14
  9.5 13.4 %all-to-all-start.1 = ((bf16[64,8,256]{2,1,0:T(8,128)(2,1)}), bf16[64,8,256]{2,1,0:T(8,128)(2,1)S(1)}, u32[]{:S(2)}, u32[]{:S(2)}) async-start(bf16[64,8,256]{2,1,0:T(8,128)(2,1)} %copy.14), calls=%async_computation.1 | async-start | bytes 524288 | tf_op jit(solution)/shard_map/all_to_all | solution.py:96
  23.0 1.7 %fusion.16 = (bf16[256,256]{1,0:T(8,128)(2,1)S(1)}, bf16[256,256]{1,0:T(8,128)(2,1)}) fusion(), kind=kLoop, calls=%fused_computation.33 | loop fusion | flops 1048576 | bytes 262144 | tf_op jit(solution)/shard_map/convert_element_type | solution.py:38
  24.7 0.1 copy.15
  24.8 1.7 %multiply_convert_fusion = (bf16[256,256]{1,0:T(8,128)(2,1)}, bf16[256,256]{1,0:T(8,128)(2,1)S(1)}) fusion(), kind=kLoop, calls=%fused_computation.17 | loop fusion | flops 1179648 | bytes 262144 | tf_op jit(solution)/shard_map/convert_element_type | solution.py:40
  26.5 0.1 copy.19
  26.6 1.0 fusion.18
  27.6 0.1 copy.16
  27.7 1.0 fusion.19
  28.7 0.1 copy.20
  28.8 1.1 %copy.13 = bf16[8,128,256]{1,0,2:T(8,128)(2,1)} copy(bf16[8,128,256]{2,1,0:T(8,128)(2,1)S(1)} %bitcast.46) | data formatting | bytes 1048576 | tf_op jit(solution)/shard_map/reshape | solution.py:90
  29.9 7.4 %all-to-all-done.1 = bf16[64,8,256]{2,1,0:T(8,128)(2,1)S(1)} async-done(((bf16[64,8,256]{2,1,0:T(8,128)(2,1)}), bf16[64,8,256]{2,1,0:T(8,128)(2,1)S(1)}, u32[]{:S(2)}, u32[]{:S(2)}) %all-to-all-start.1) | async-done | bytes 262176 | tf_op jit(solution)/shard_map/all_to_all | solution.py:96
  37.3 0.7 copy-done.2
  38.0 11.5 %all-to-all-start = ((bf16[256,8,128]{2,1,0:T(8,128)(2,1)}), bf16[256,8,128]{2,1,0:T(8,128)(2,1)S(1)}, u32[]{:S(2)}, u32[]{:S(2)}) async-start(bf16[256,8,128]{2,1,0:T(8,128)(2,1)} %bitcast.1), calls=%async_computation | async-start | bytes 1048576 | tf_op jit(solution)/shard_map/all_to_all | solution.py:91
  49.4 1.9 %broadcast_multiply_fusion.1 = (bf16[2,256,256,2]{1,0,3,2:T(2,128)(2,1)S(1)}, bf16[2,256,256,2]{1,0,3,2:T(2,128)(2,1)S(1)}, bf16[2,256,256,2]{1,0,3,2:T(2,128)(2,1)S(1)}, bf16[2,256,256,2]{1,0,3,2:T(2,128)(2,1)S(1)}) fusion(bf16[256,256]{0,1:T(8,128)(2,1)S(1)} %copy.19, bf16[2,2]{0,1:T(2,128)(2,1)S(1)} %compare_convert_fusion, ...), kind=kLoop, calls=%fused_computation.16 | loop fusion | flops 1048576 | bytes 2621448 | tf_op jit(solution)/shard_map/mul | solution.py:32
  51.6 0.2 copy.17
  51.8 0.1 copy.23
  51.9 0.2 copy.18
  52.2 0.3 copy-done.5
  52.5 0.6 dynamic_slice.3.gain
  53.2 1.8 %fusion.12 = (f32[256,256]{1,0:T(8,128)}, f32[256,256]{1,0:T(8,128)}) fusion(), kind=kLoop, calls=%fused_computation.29 | loop fusion | flops 917504 | bytes 524288 | tf_op jit(solution)/shard_map/sin | solution.py:27
  54.9 1.8 %maximum_maximum_fusion.second = bf16[512,512]{1,0:T(8,128)(2,1)} fusion(bf16[256,256]{1,0:T(8,128)(2,1)S(1)} %get-tuple-element.9, bf16[256,256]{1,0:T(8,128)(2,1)} %get-tuple-element.10, bf16[256,256]{1,0:T(8,128)(2,1)} %copy-done.1), kind=kLoop, calls=%fused_computation.4 | loop fusion | flops 2097152 | bytes 917504 | tf_op jit(solution)/shard_map/concatenate | solution.py:42
  56.7 0.8 maximum_maximum_fusion.1.third
  57.6 1.2 %pad_maximum_fusion.1.fourth = bf16[512,1024]{1,0:T(8,128)(2,1)} fusion(bf16[512,512]{1,0:T(8,128)(2,1)S(1)} %bitcast.37, bf16[512,512]{1,0:T(8,128)(2,1)S(1)} %bitcast.36), kind=kLoop, calls=%fused_computation.1 | loop fusion | flops 2097152 | bytes 2097152 | tf_op jit(solution)/shard_map/concatenate | solution.py:48
  58.7 1.0 pad_maximum_fusion.first
  59.8 1.0 fusion.order
  60.7 7.3 %all-to-all-done = bf16[256,8,128]{2,1,0:T(8,128)(2,1)S(1)} async-done(((bf16[256,8,128]{2,1,0:T(8,128)(2,1)}), bf16[256,8,128]{2,1,0:T(8,128)(2,1)S(1)}, u32[]{:S(2)}, u32[]{:S(2)}) %all-to-all-start) | async-done | bytes 524320 | tf_op jit(solution)/shard_map/all_to_all | solution.py:91
  68.1 0.8 copy-done
  68.8 7.8 %shard_map.37 = bf16[4,512,128]{2,1,0:T(8,128)(2,1)} custom-call(f32[1]{0:T(128)} %dynamic_slice.3.gain, bf16[4,512,128]{2,1,0:T(8,128)(2,1)} %bitcast.42, bf16[512,256]{1,0:T(8,128)(2,1)} %bitcast.44, bf16[512,512]{1,0:T(8,128)(2,1)} %fusion.order, bf16[1024,512]{1,0:T(8,128)(2,1)} %pad_maximum_fusion.first, bf16[512,512]{1,0:T(8,128)(2,1)} %maximum_maximum_fusion.second, ...), custom_call_target="tpu_custom_call" | custom-call | tf_op jit(solution)/shard_map/pallas_call | solution.py:102
  76.6 27.6 %all_to_all.15 = bf16[256,8,128]{2,1,0:T(8,128)(2,1)S(1)} all-to-all(bf16[256,8,128]{2,1,0:T(8,128)(2,1)} %bitcast.43), channel_id=1, replica_groups=mesh['seq'=64,'ylo'=4,'core'=2] {'ylo','seq'}, dimensions={0} | all-to-all | bytes 1048576 | tf_op jit(solution)/shard_map/all_to_all | solution.py:109
  104.2 1.1 %copy.21 = bf16[8,128,256]{2,1,0:T(8,128)(2,1)} copy(bf16[8,128,256]{1,0,2:T(8,128)(2,1)S(1)} %bitcast.35) | data formatting | bytes 1048576 | tf_op jit(solution)/shard_map/transpose | solution.py:110
  (14 shorter events, 0.3 us)
Async XLA Ops:
  9.5 27.7 %all-to-all-start.1 = ((bf16[64,8,256]{2,1,0:T(8,128)(2,1)}), bf16[64,8,256]{2,1,0:T(8,128)(2,1)S(1)}, u32[]{:S(2)}, u32[]{:S(2)}) async-start(bf16[64,8,256]{2,1,0:T(8,128)(2,1)} %copy.14), calls=%async_computation.1 | async-start | bytes 524288 | tf_op jit(solution)/shard_map/all_to_all | solution.py:96
  22.9 5.9 %copy-start.4 = (bf16[1,1024,256]{2,1,0:T(8,128)(2,1)S(1)}, bf16[1,1024,256]{2,1,0:T(8,128)(2,1)}, u32[]{:S(2)}) copy-start(bf16[1,1024,256]{2,1,0:T(8,128)(2,1)} %param.3) | copy-start | bytes 1572868
  27.6 9.7 %copy-start.1 = (bf16[256,256]{1,0:T(8,128)(2,1)}, bf16[256,256]{1,0:T(8,128)(2,1)S(1)}, u32[]{:S(2)}) copy-start(bf16[256,256]{1,0:T(8,128)(2,1)S(1)} %fusion.18) | copy-start | bytes 393220
  37.3 0.7 copy-start.2
  38.0 30.1 %all-to-all-start = ((bf16[256,8,128]{2,1,0:T(8,128)(2,1)}), bf16[256,8,128]{2,1,0:T(8,128)(2,1)S(1)}, u32[]{:S(2)}, u32[]{:S(2)}) async-start(bf16[256,8,128]{2,1,0:T(8,128)(2,1)} %bitcast.1), calls=%async_computation | async-start | bytes 1048576 | tf_op jit(solution)/shard_map/all_to_all | solution.py:91
  51.8 0.7 copy-start.5
  52.2 4.6 %copy-start.3 = (bf16[256,256]{1,0:T(8,128)(2,1)S(1)}, bf16[256,256]{1,0:T(8,128)(2,1)}, u32[]{:S(2)}) copy-start(bf16[256,256]{1,0:T(8,128)(2,1)} %get-tuple-element.11) | copy-start | bytes 393220
  68.1 0.8 copy-start

commit v2 on v1

--- a/solution.py
+++ b/solution.py
@@ -11,6 +11,7 @@
 N1 = 256
 N2 = 256
 HALF = 128
+TOKEN_GROUP = ("ylo", "yh", "xz")
 
 
 def cos_sin(points):
@@ -86,14 +87,18 @@
 
 def body(tokens, filter_spectrum, skip_gain):
     channels = tokens.shape[-1]
-    channel = lax.axis_index("ylo") * lax.axis_size("seq") + lax.axis_index("seq")
+    channel = lax.axis_index(("ylo", "yh", "xz"))
     laid_out = tokens.reshape(8, HALF, channels).transpose(2, 0, 1)
-    u = lax.all_to_all(laid_out, ("ylo", "seq"), split_axis=0, concat_axis=0, tiled=True)
+    with jax.named_scope("tok"):
+        u = lax.all_to_all(laid_out, TOKEN_GROUP, split_axis=0, concat_axis=0, tiled=True)
     u = u.reshape(4, 2 * N1, HALF)
-    mine = filter_spectrum.transpose(3, 0, 1, 2)
-    both = lax.all_gather(mine, "core", axis=0, tiled=True)
-    both = both.reshape(both.shape[0], 8, N2)
-    filt = lax.all_to_all(both, "seq", split_axis=0, concat_axis=0, tiled=True)
+    mine = filter_spectrum.transpose(3, 0, 1, 2).reshape(32, 8, N2)
+    with jax.named_scope("flt"):
+        mine = lax.all_to_all(mine, "xz", split_axis=0, concat_axis=0, tiled=True)
+        with jax.named_scope("turn"):
+            mine = lax.ppermute(mine, ("yh", "core"), [(0, 0), (1, 2), (2, 1), (3, 3)])
+        with jax.named_scope("pair"):
+            filt = lax.all_gather(mine, "core", axis=0, tiled=True)
     filt = filt.reshape(2 * N1, N2)
     gain = lax.dynamic_slice(skip_gain, (channel,), (1,))
     first, second, third, fourth = tables()
@@ -106,16 +111,16 @@
         out_specs=vmem,
     )(gain, u, filt, row_order(), first, second, third, fourth, cos_tw, sin_tw)
     mixed = mixed.reshape(4 * 64, 8, HALF)
-    back = lax.all_to_all(mixed, ("ylo", "seq"), split_axis=0, concat_axis=0, tiled=True)
+    back = lax.all_to_all(mixed, TOKEN_GROUP, split_axis=0, concat_axis=0, tiled=True)
     return back.transpose(1, 2, 0).reshape(1, 8 * HALF, channels)
 
 
 def solution(mesh):
     names = mesh.axis_names
     assert names == ("seq", "bat")
-    split = Mesh(mesh.devices.reshape(64, 4, 2), ("seq", "ylo", "core"))
-    bat = ("ylo", "core")
-    placed = (P(bat, "seq", None), P(None, "seq", None, bat), P())
+    split = Mesh(mesh.devices.reshape(2, 32, 4, 2), ("yh", "xz", "ylo", "core"))
+    bat, seq = ("ylo", "core"), ("yh", "xz")
+    placed = (P(bat, seq, None), P(None, seq, None, bat), P())
     return jax.shard_map(
-        body, mesh=split, in_specs=placed, out_specs=P(bat, "seq", None), check_vma=False
+        body, mesh=split, in_specs=placed, out_specs=P(bat, seq, None), check_vma=False
     )

time: 107 us -> 109 us (1.019); the launches traced: 105 us -> 109 us
  starting transfers between devices: 24.9 us -> 39.7 us
  waiting for transfers between devices: 14.7 us -> 1.84 us
  blocking collectives: 36.3 us -> 39.5 us
  other arithmetic: 14.9 us -> 12.7 us
    all_to_all x2, waiting for transfers between devices: 14.7 us -> 0.17 us  [the longest x1 0.17 us: body(): lax.all_to_all(laid_out, TOKEN_GROUP, split_axis=0, concat_axis=0, tiled=...]
    all_to_all x1, blocking collectives: 27.6 us -> 37.2 us  [body(): lax.all_to_all(mixed, TOKEN_GROUP, split_axis=0, concat_axis=0, tiled=True)]
    all_to_all x2, starting transfers between devices: 24.9 us -> 32.4 us  [the longest x1 18.7 us: body(): lax.all_to_all(laid_out, TOKEN_GROUP, split_axis=0, concat_axis=0, tiled=...]
    ppermute x0 -> x1, starting transfers between devices: none -> 7.28 us  [body(): mine = lax.ppermute(mine, ('yh', 'core'), [(0, 0), (1, 2), (2, 1), (3, 3)])]
    all_gather x1, blocking collectives: 8.67 us -> 2.29 us  [body(): filt = lax.all_gather(mine, 'core', axis=0, tiled=True)]
    ppermute x0 -> x1, waiting for transfers between devices: none -> 1.67 us  [body(): mine = lax.ppermute(mine, ('yh', 'core'), [(0, 0), (1, 2), (2, 1), (3, 3)])]
    unnamed x16 -> x8, local copies, waits for them, and re-layouts: 2.19 us -> 1.13 us
  transfers between devices with their start and end apart: 2 -> 3, of which waited for: 2 -> 2; matrix products, arithmetic and copies ran while one was open for 17% -> 15% of each run, Pallas kernels for 0% -> 0%
where the time goes in v2:
time: 109 us
  starting transfers between devices  39.7 us (36%)
  blocking collectives  39.5 us (36%)
  other arithmetic  12.7 us (12%)
  Pallas kernels  7.75 us (7%)
  local copies, waits for them, and re-layouts  7.44 us (7%)
  waiting for transfers between devices  1.84 us (2%)
    all_to_all x1, blocking collectives, body(): lax.all_to_all(mixed, TOKEN_GROUP, split_axis=0, concat_axis=0, tiled=True)  37.2 us
    all_to_all x1, starting transfers between devices, body(): lax.all_to_all(laid_out, TOKEN_GROUP, split_axis=0, concat_axis=0, tiled=...  18.7 us
    all_to_all x1, starting transfers between devices, body(): mine = lax.all_to_all(mine, 'xz', split_axis=0, concat_axis=0, tiled=True)  13.7 us
    pallas_call x1, Pallas kernels, body(): pl.pallas_call(convolve, out_shape=jax.ShapeDtypeStruct((4, 2 * N1, HALF)...  7.75 us
    ppermute x1, starting transfers between devices, body(): mine = lax.ppermute(mine, ('yh', 'core'), [(0, 0), (1, 2), (2, 1), (3, 3)])  7.28 us
    all_gather x1, blocking collectives, body(): filt = lax.all_gather(mine, 'core', axis=0, tiled=True)  2.29 us
  transfers between devices with their start and end apart: 3, of which 2 were waited for; matrix products, arithmetic and copies ran while one was open for 15% of the time, Pallas kernels for 0%

profile of v2, /device:TPU:1, one launch (start us, length us, event | category | flops | bytes accessed | tf_op | source)
XLA Modules:
  0.0 109.0 jit_solution(938035297260952930)
XLA Ops:
  0.0 1.6 %copy.31 = bf16[32,8,256]{2,1,0:T(8,128)(2,1)} copy(bf16[32,8,256]{2,0,1:T(8,128)(2,1)} %bitcast.47) | data formatting | bytes 262144 | tf_op jit(solution)/shard_map/reshape | solution.py:95
  1.6 13.7 %all-to-all-start.1 = ((bf16[32,8,256]{2,1,0:T(8,128)(2,1)}), bf16[32,8,256]{2,1,0:T(8,128)(2,1)S(1)}, u32[]{:S(2)}, u32[]{:S(2)}) async-start(bf16[32,8,256]{2,1,0:T(8,128)(2,1)} %copy.31), calls=%async_computation.1 | async-start | bytes 262144 | tf_op jit(solution)/shard_map/flt/all_to_all | solution.py:97
  15.3 1.1 %fusion.16 = (bf16[256,256]{1,0:T(8,128)(2,1)S(1)}, bf16[256,256]{1,0:T(8,128)(2,1)S(1)}) fusion(), kind=kLoop, calls=%fused_computation.33 | loop fusion | flops 1048576 | bytes 262144 | tf_op jit(solution)/shard_map/convert_element_type | solution.py:39
  16.4 1.1 %multiply_convert_fusion = (bf16[256,256]{1,0:T(8,128)(2,1)S(1)}, bf16[256,256]{1,0:T(8,128)(2,1)S(1)}) fusion(), kind=kLoop, calls=%fused_computation.17 | loop fusion | flops 1179648 | bytes 262144 | tf_op jit(solution)/shard_map/convert_element_type | solution.py:41
  17.6 1.0 fusion.18
  18.6 1.0 fusion.19
  19.6 0.1 copy.24
  19.7 0.1 copy.28
  19.8 0.1 copy.25
  19.9 0.1 copy.29
  20.0 1.9 %broadcast_multiply_fusion.1 = (bf16[2,256,256,2]{1,0,3,2:T(2,128)(2,1)S(1)}, bf16[2,256,256,2]{1,0,3,2:T(2,128)(2,1)S(1)}, bf16[2,256,256,2]{1,0,3,2:T(2,128)(2,1)S(1)}, bf16[2,256,256,2]{1,0,3,2:T(2,128)(2,1)S(1)}) fusion(bf16[256,256]{0,1:T(8,128)(2,1)S(1)} %copy.28, bf16[2,2]{0,1:T(2,128)(2,1)S(1)} %compare_convert_fusion, ...), kind=kLoop, calls=%fused_computation.16 | loop fusion | flops 1048576 | bytes 2621448 | tf_op jit(solution)/shard_map/mul | solution.py:33
  21.9 0.1 copy.34
  22.0 0.1 copy.35
  22.2 0.2 copy.26
  22.5 0.2 copy.27
  22.7 2.1 %copy.22 = bf16[8,128,256]{1,0,2:T(8,128)(2,1)} copy(bf16[8,128,256]{2,1,0:T(8,128)(2,1)} %bitcast.46) | data formatting | bytes 1048576 | tf_op jit(solution)/shard_map/reshape | solution.py:91
  24.8 18.7 %all-to-all-start = ((bf16[256,8,128]{2,1,0:T(8,128)(2,1)}), bf16[256,8,128]{2,1,0:T(8,128)(2,1)S(1)}, u32[]{:S(2)}, u32[]{:S(2)}) async-start(bf16[256,8,128]{2,1,0:T(8,128)(2,1)} %bitcast.1), calls=%async_computation | async-start | bytes 1048576 | tf_op jit(solution)/shard_map/tok/all_to_all | solution.py:93
  43.5 1.8 %fusion.12 = (f32[256,256]{1,0:T(8,128)}, f32[256,256]{1,0:T(8,128)}) fusion(), kind=kLoop, calls=%fused_computation.29 | loop fusion | flops 917504 | bytes 524288 | tf_op jit(solution)/shard_map/sin | solution.py:28
  45.3 1.2 %pad_maximum_fusion.1.fourth = bf16[512,1024]{1,0:T(8,128)(2,1)} fusion(bf16[512,512]{1,0:T(8,128)(2,1)S(1)} %bitcast.38, bf16[512,512]{1,0:T(8,128)(2,1)S(1)} %bitcast.37), kind=kLoop, calls=%fused_computation.1 | loop fusion | flops 2097152 | bytes 2097152 | tf_op jit(solution)/shard_map/concatenate | solution.py:49
  46.5 1.0 pad_maximum_fusion.first
  47.5 1.0 fusion.order
  48.5 7.3 %collective-permute-start = (bf16[32,8,256]{2,1,0:T(8,128)(2,1)S(1)}, bf16[32,8,256]{2,1,0:T(8,128)(2,1)S(1)}, u32[]{:S(2)}, u32[]{:S(2)}) collective-permute-start(bf16[32,8,256]{2,1,0:T(8,128)(2,1)S(1)} %all-to-all-done.1), channel_id=1, source_target_pairs={{0,0},{1,256},{256,1},{257,257},{2,2},{3,258},{258,3},{259,259},{4... | collective-permute-start | bytes 393224 | tf_op jit(solution)/shard_map/flt/turn/ppermute | solution.py:99
  55.8 0.8 maximum_maximum_fusion.second
  56.6 0.6 dynamic_slice.3.gain
  57.2 0.8 maximum_maximum_fusion.1.third
  58.1 1.7 %collective-permute-done = bf16[32,8,256]{2,1,0:T(8,128)(2,1)S(1)} collective-permute-done((bf16[32,8,256]{2,1,0:T(8,128)(2,1)S(1)}, bf16[32,8,256]{2,1,0:T(8,128)(2,1)S(1)}, u32[]{:S(2)}, u32[]{:S(2)}) %collective-permute-start) | collective-permute-done | bytes 131104 | tf_op jit(solution)/shard_map/flt/turn/ppermute | solution.py:99
  59.8 2.3 %all_gather.3 = bf16[64,8,256]{2,1,0:T(8,128)(2,1)} all-gather(bf16[32,8,256]{2,1,0:T(8,128)(2,1)S(1)} %collective-permute-done), channel_id=1, replica_groups=mesh['yh'=2,'xz'=32,'ylo'=4,'core'=2] {'core'}, dimensions={0}, use_global_device_ids=true | all-gather | bytes 393216 | tf_op jit(solution)/shard_map/flt/pair/all_gather | solution.py:101
  62.0 0.2 all-to-all-done
  62.2 0.8 copy-done
  63.0 7.7 %shard_map.37 = bf16[4,512,128]{2,1,0:T(8,128)(2,1)} custom-call(f32[1]{0:T(128)} %dynamic_slice.3.gain, bf16[4,512,128]{2,1,0:T(8,128)(2,1)} %bitcast.43, bf16[512,256]{1,0:T(8,128)(2,1)} %bitcast.45, bf16[512,512]{1,0:T(8,128)(2,1)} %fusion.order, bf16[1024,512]{1,0:T(8,128)(2,1)} %pad_maximum_fusion.first, bf16[512,512]{1,0:T(8,128)(2,1)} %maximum_maximum_fusion.second, ...), custom_call_target="tpu_custom_call" | custom-call | tf_op jit(solution)/shard_map/pallas_call | solution.py:107
  70.8 37.2 %all_to_all.15 = bf16[256,8,128]{2,1,0:T(8,128)(2,1)S(1)} all-to-all(bf16[256,8,128]{2,1,0:T(8,128)(2,1)} %bitcast.44), channel_id=1, replica_groups=mesh['yh'=2,'xz'=32,'ylo'=4,'core'=2] {'ylo','yh','xz'}, dimensions={0} | all-to-all | bytes 1048576 | tf_op jit(solution)/shard_map/all_to_all | solution.py:114
  107.9 1.1 %copy.30 = bf16[8,128,256]{2,1,0:T(8,128)(2,1)} copy(bf16[8,128,256]{1,0,2:T(8,128)(2,1)S(1)} %bitcast.36) | data formatting | bytes 1048576 | tf_op jit(solution)/shard_map/transpose | solution.py:115
  (8 shorter events, 0.2 us)
Async XLA Ops:
  1.6 23.2 %all-to-all-start.1 = ((bf16[32,8,256]{2,1,0:T(8,128)(2,1)}), bf16[32,8,256]{2,1,0:T(8,128)(2,1)S(1)}, u32[]{:S(2)}, u32[]{:S(2)}) async-start(bf16[32,8,256]{2,1,0:T(8,128)(2,1)} %copy.31), calls=%async_computation.1 | async-start | bytes 262144 | tf_op jit(solution)/shard_map/flt/all_to_all | solution.py:97
  24.8 37.4 %all-to-all-start = ((bf16[256,8,128]{2,1,0:T(8,128)(2,1)}), bf16[256,8,128]{2,1,0:T(8,128)(2,1)S(1)}, u32[]{:S(2)}, u32[]{:S(2)}) async-start(bf16[256,8,128]{2,1,0:T(8,128)(2,1)} %bitcast.1), calls=%async_computation | async-start | bytes 1048576 | tf_op jit(solution)/shard_map/tok/all_to_all | solution.py:93
  47.5 9.1 %copy-start.1 = (f32[256]{0:T(256)S(1)}, f32[256]{0:T(256)}, u32[]{:S(2)}) copy-start(f32[256]{0:T(256)} %param.5) | copy-start | bytes 3076
  48.5 11.3 %collective-permute-start = (bf16[32,8,256]{2,1,0:T(8,128)(2,1)S(1)}, bf16[32,8,256]{2,1,0:T(8,128)(2,1)S(1)}, u32[]{:S(2)}, u32[]{:S(2)}) collective-permute-start(bf16[32,8,256]{2,1,0:T(8,128)(2,1)S(1)} %all-to-all-done.1), channel_id=1, source_target_pairs={{0,0},{1,256},{256,1},{257,257},{2,2},{3,258},{258,3},{259,259},{4... | collective-permute-start | bytes 393224 | tf_op jit(solution)/shard_map/flt/turn/ppermute | solution.py:99
  62.2 0.8 copy-start

commit v3 on v2

v3 whole, which is shorter than its diff:
```python
import math

import jax
import jax.numpy as jnp
from jax import lax
from jax.experimental import pallas as pl
from jax.experimental.pallas import tpu as pltpu
from jax.sharding import Mesh
from jax.sharding import PartitionSpec as P


N1 = 256
N2 = 256
HALF = 128
TOKEN_GROUP = ("ylo", "yh", "xz")
VMEM = pl.BlockSpec(memory_space=pltpu.VMEM)
HBM = pl.BlockSpec(memory_space=pltpu.HBM)
KERNEL = pltpu.CompilerParams(vmem_limit_bytes=24 * 1024 * 1024)


def grid_of(shape, dim):
    return lax.broadcasted_iota(jnp.int32, shape, dim)


def make_tables(first, second, fourth, cos_tw, sin_tw, order):
    def cos_sin(period):
        square = (N1, N2)
        index_grid = grid_of(square, 0) * grid_of(square, 1) % period
        angle = index_grid.astype(jnp.float32) * (2.0 * math.pi / period)
        return jnp.cos(angle), jnp.sin(angle)

    c, s = cos_sin(N1)
    c16, s16, n16 = c.astype(jnp.bfloat16), s.astype(jnp.bfloat16), (-s).astype(jnp.bfloat16)
    second[:N2, :N2] = c16
    second[:N2, N2:] = n16
    second[N2:, :N2] = s16
    second[N2:, N2:] = c16
    tall, wide = jnp.concatenate([c16, n16], axis=0), jnp.concatenate([c16, n16], axis=1)
    for half in range(2):
        spread = (N1, 2 * N1)
        pick = jnp.where(grid_of(spread, 1) == 2 * grid_of(spread, 0) + half, 1.0, 0.0).astype(jnp.bfloat16)
        block = dot(tall, pick).astype(jnp.bfloat16)
        first[half * N1 : (half + 1) * N1, :] = block[:N1]
        first[(2 + half) * N1 : (3 + half) * N1, :] = block[N1:]
        spread = (2 * N1, N1)
        pick = jnp.where(grid_of(spread, 0) == 2 * grid_of(spread, 1) + half, 1.0, 0.0).astype(jnp.bfloat16)
        block = dot(pick, wide).astype(jnp.bfloat16)
        fourth[:, half * N1 : (half + 1) * N1] = block[:, :N1]
        fourth[:, (2 + half) * N1 : (3 + half) * N1] = block[:, N1:]
    c, s = cos_sin(N1 * N2)
    cos_tw[...] = c
    sin_tw[...] = s
    full = (2 * N1, 2 * N1)
    want = grid_of(full, 0)
    part, k1 = want // N1, want % N1
    source = (k1 // 4) * 8 + part * 4 + k1 % 4
    order[...] = jnp.where(source == grid_of(full, 1), 1.0, 0.0).astype(jnp.bfloat16)


def dot(a, b):
    return jnp.dot(a, b, preferred_element_type=jnp.float32)


def convolve(gain, u, filt, first, fourth, second_hbm, cos_hbm, sin_hbm, order_hbm, out, second, cos_tw, sin_tw, order, arrived):
    late = ((cos_hbm, cos_tw), (sin_hbm, sin_tw), (second_hbm, second), (order_hbm, order))
    copies = [pltpu.make_async_copy(far, near, arrived.at[i]) for i, (far, near) in enumerate(late)]
    for copy in copies:
        copy.start()
    batches = u.shape[0]
    section = dot(first[...], jnp.concatenate([u[b] for b in range(batches)], axis=1))
    for copy in copies:
        copy.wait()
    c, s = cos_tw[...], sin_tw[...]
    weights = dot(order[...], filt[...])
    wr, wi = weights[:N1], weights[N1:]
    for b in range(batches):
        lanes = slice(b * HALF, (b + 1) * HALF)
        piece = section[:, lanes]
        re = jnp.concatenate([piece[:N1], piece[N1 : 2 * N1]], axis=1)
        im = jnp.concatenate([piece[2 * N1 : 3 * N1], piece[3 * N1 :]], axis=1)
        turned = jnp.concatenate([re * c + im * s, im * c - re * s], axis=1).astype(jnp.bfloat16)
        spectrum = dot(turned, second[...])
        sr, si = spectrum[:, :N2], spectrum[:, N2:]
        product = jnp.concatenate([sr * wr - si * wi, -(sr * wi) - si * wr], axis=1).astype(jnp.bfloat16)
        back = dot(product, second[...])
        br, nbi = back[:, :N2], back[:, N2:]
        tr = (br * c + nbi * s).astype(jnp.bfloat16)
        ti = (br * s - nbi * c).astype(jnp.bfloat16)
        rows = jnp.concatenate([tr[:, :HALF], tr[:, HALF:], ti[:, :HALF], ti[:, HALF:]], axis=0)
        filtered = dot(fourth[...], rows) * (1.0 / (N1 * N2))
        out[b] = (filtered + gain[0] * u[b].astype(jnp.float32)).astype(jnp.bfloat16)


def layer(tokens, filter_spectrum, skip_gain):
    channels = tokens.shape[-1]
    channel = lax.axis_index(TOKEN_GROUP)
    laid_out = tokens.reshape(8, HALF, channels).transpose(2, 0, 1)
    u = lax.all_to_all(laid_out, TOKEN_GROUP, split_axis=0, concat_axis=0, tiled=True)
    u = u.reshape(4, 2 * N1, HALF)
    mine = filter_spectrum.transpose(3, 0, 1, 2).reshape(32, 8, N2)
    mine = lax.all_to_all(mine, "xz", split_axis=0, concat_axis=0, tiled=True)
    mine = lax.ppermute(mine, ("yh", "core"), [(0, 0), (1, 2), (2, 1), (3, 3)])
    filt = lax.all_gather(mine, "core", axis=0, tiled=True)
    filt = filt.reshape(2 * N1, N2)
    gain = lax.dynamic_slice(skip_gain, (channel,), (1,))
    first, second, fourth, cos_tw, sin_tw, order = pl.pallas_call(
        make_tables,
        out_shape=[
            jax.ShapeDtypeStruct((4 * N1, 2 * N1), jnp.bfloat16),
            pltpu.HBM((2 * N2, 2 * N2), jnp.bfloat16),
            jax.ShapeDtypeStruct((2 * N1, 4 * N1), jnp.bfloat16),
            pltpu.HBM((N1, N2), jnp.float32),
            pltpu.HBM((N1, N2), jnp.float32),
            pltpu.HBM((2 * N1, 2 * N1), jnp.bfloat16),
        ],
        out_specs=[VMEM, VMEM, VMEM, VMEM, VMEM, VMEM],
        compiler_params=KERNEL,
    )()
    second, cos_tw, sin_tw, order = (
        pltpu.with_memory_space_constraint(table, pltpu.HBM) for table in (second, cos_tw, sin_tw, order)
    )
    mixed = pl.pallas_call(
        convolve,
        out_shape=jax.ShapeDtypeStruct((4, 2 * N1, HALF), jnp.bfloat16),
        in_specs=[pl.BlockSpec(memory_space=pltpu.SMEM)] + [VMEM] * 4 + [HBM] * 4,
        out_specs=VMEM,
        scratch_shapes=[
            pltpu.VMEM((2 * N2, 2 * N2), jnp.bfloat16),
            pltpu.VMEM((N1, N2), jnp.float32),
            pltpu.VMEM((N1, N2), jnp.float32),
            pltpu.VMEM((2 * N1, 2 * N1), jnp.bfloat16),
            pltpu.SemaphoreType.DMA((4,)),
        ],
        compiler_params=KERNEL,
    )(gain, u, filt, first, fourth, second, cos_tw, sin_tw, order)
    mixed = mixed.reshape(4 * 64, 8, HALF)
    back = lax.all_to_all(mixed, TOKEN_GROUP, split_axis=0, concat_axis=0, tiled=True)
    return back.transpose(1, 2, 0).reshape(1, 8 * HALF, channels)


def solution(mesh):
    split = Mesh(mesh.devices.reshape(2, 32, 4, 2), ("yh", "xz", "ylo", "core"))
    bat, seq = ("ylo", "core"), ("yh", "xz")
    placed = (P(bat, seq, None), P(None, seq, None, bat), P())
    return jax.shard_map(layer, mesh=split, in_specs=placed, out_specs=P(bat, seq, None), check_vma=False)
```

time: 109 us -> 98.5 us (0.904)
  other arithmetic: 12.7 us -> 0 us
  waiting for transfers between devices: 1.84 us -> 11.6 us
  starting transfers between devices: 39.7 us -> 34.8 us
  blocking collectives: 39.5 us -> 36.6 us
  local copies, waits for them, and re-layouts: 7.44 us -> 5.18 us
  Pallas kernels: 7.75 us -> 9.83 us
    all_to_all x2, waiting for transfers between devices: 0.17 us -> 8.32 us  [the longest x1 8.07 us: layer(): mine = lax.all_to_all(mine, 'xz', split_axis=0, concat_axis=0, tiled=True)]
    all_to_all x2, starting transfers between devices: 32.4 us -> 26.9 us  [the longest x1 13.7 us: layer(): mine = lax.all_to_all(mine, 'xz', split_axis=0, concat_axis=0, tiled=True)]
    concatenate x4 -> x0, other arithmetic: 3.89 us -> none  [the longest x1 1.17 us: tables(): fourth = jnp.concatenate([spread_rows(ci).T, spread_rows(-si).T], axis=1)]
    convert_element_type x4 -> x0, other arithmetic: 3.17 us -> none  [the longest x1 1.11 us: tables(): si = (sine / N1).astype(jnp.bfloat16)]
    all_to_all x1, blocking collectives: 37.2 us -> 34.7 us  [layer(): lax.all_to_all(mixed, TOKEN_GROUP, split_axis=0, concat_axis=0, tiled=True)]
    pallas_call x1 -> x2, Pallas kernels: 7.75 us -> 9.83 us  [the longest x1 6.26 us: layer(): pl.pallas_call(convolve, out_shape=jax.ShapeDtypeStruct((4, 2 * N1, HALF)...]
    neg x2 -> x0, other arithmetic: 1.98 us -> none  [the longest x1 0.99 us: tables(): first = jnp.concatenate([spread_rows(c16), spread_rows(-s16)], axis=0)]
    mul x1 -> x0, other arithmetic: 1.89 us -> none  [spread_rows(): wide = eye[:, None, None, :] * table[None, :, :, None]]
  transfers between devices with their start and end apart: 3 -> 3, of which waited for: 2 -> 3; matrix products, arithmetic and copies ran while one was open for 15% -> 2% of each run, Pallas kernels for 0% -> 4%
where the time goes in v3:
time: 98.5 us; the launch traced here: 98.1 us
  blocking collectives  36.6 us (37%)
  starting transfers between devices  34.8 us (35%)
  waiting for transfers between devices  11.6 us (12%)
  Pallas kernels  9.83 us (10%)
  local copies, waits for them, and re-layouts  5.18 us (5%)
    all_to_all x1, blocking collectives, layer(): lax.all_to_all(mixed, TOKEN_GROUP, split_axis=0, concat_axis=0, tiled=True)  34.7 us
    all_to_all x1, starting transfers between devices, layer(): mine = lax.all_to_all(mine, 'xz', split_axis=0, concat_axis=0, tiled=True)  13.7 us
    all_to_all x1, starting transfers between devices, layer(): lax.all_to_all(laid_out, TOKEN_GROUP, split_axis=0, concat_axis=0, tiled=...  13.2 us
    all_to_all x1, waiting for transfers between devices, layer(): mine = lax.all_to_all(mine, 'xz', split_axis=0, concat_axis=0, tiled=True)  8.07 us
    ppermute x1, starting transfers between devices, layer(): mine = lax.ppermute(mine, ('yh', 'core'), [(0, 0), (1, 2), (2, 1), (3, 3)])  7.9 us
    pallas_call x1, Pallas kernels, layer(): pl.pallas_call(convolve, out_shape=jax.ShapeDtypeStruct((4, 2 * N1, HALF)...  6.26 us
    pallas_call x1, Pallas kernels, layer(): pl.pallas_call(make_tables, out_shape=[jax.ShapeDtypeStruct((4 * N1, 2 *...  3.57 us
    ppermute x1, waiting for transfers between devices, layer(): mine = lax.ppermute(mine, ('yh', 'core'), [(0, 0), (1, 2), (2, 1), (3, 3)])  3.29 us
  transfers between devices with their start and end apart: 3, of which 3 were waited for; matrix products, arithmetic and copies ran while one was open for 2% of the time, Pallas kernels for 4%

profile of v3, /device:TPU:1, one launch (start us, length us, event | category | flops | bytes accessed | tf_op | source)
XLA Modules:
  0.0 98.1 jit_solution(9297135086411694295)
XLA Ops:
  0.0 0.0 copy-start
  0.0 1.7 %copy.10 = bf16[32,8,256]{2,1,0:T(8,128)(2,1)} copy(bf16[32,8,256]{2,0,1:T(8,128)(2,1)} %bitcast.15) | data formatting | bytes 262144 | tf_op jit(solution)/shard_map/reshape | solution.py:100
  1.7 13.7 %all-to-all-start.1 = ((bf16[32,8,256]{2,1,0:T(8,128)(2,1)}), bf16[32,8,256]{2,1,0:T(8,128)(2,1)S(1)}, u32[]{:S(2)}, u32[]{:S(2)}) async-start(bf16[32,8,256]{2,1,0:T(8,128)(2,1)} %copy.10), calls=%async_computation.1 | async-start | bytes 262144 | tf_op jit(solution)/shard_map/all_to_all | solution.py:101
  15.4 0.0 copy-done
  15.4 1.1 %copy.7 = bf16[8,128,256]{1,0,2:T(8,128)(2,1)} copy(bf16[8,128,256]{2,1,0:T(8,128)(2,1)S(1)} %bitcast.14) | data formatting | bytes 1048576 | tf_op jit(solution)/shard_map/reshape | solution.py:97
  16.5 8.1 %all-to-all-done.1 = bf16[32,8,256]{2,1,0:T(8,128)(2,1)S(1)} async-done(((bf16[32,8,256]{2,1,0:T(8,128)(2,1)}), bf16[32,8,256]{2,1,0:T(8,128)(2,1)S(1)}, u32[]{:S(2)}, u32[]{:S(2)}) %all-to-all-start.1) | async-done | bytes 131104 | tf_op jit(solution)/shard_map/all_to_all | solution.py:101
  24.6 13.2 %all-to-all-start = ((bf16[256,8,128]{2,1,0:T(8,128)(2,1)}), bf16[256,8,128]{2,1,0:T(8,128)(2,1)S(1)}, u32[]{:S(2)}, u32[]{:S(2)}) async-start(bf16[256,8,128]{2,1,0:T(8,128)(2,1)} %bitcast.1), calls=%async_computation | async-start | bytes 1048576 | tf_op jit(solution)/shard_map/all_to_all | solution.py:98
  37.8 7.9 %collective-permute-start = (bf16[32,8,256]{2,1,0:T(8,128)(2,1)S(1)}, bf16[32,8,256]{2,1,0:T(8,128)(2,1)S(1)}, u32[]{:S(2)}, u32[]{:S(2)}) collective-permute-start(bf16[32,8,256]{2,1,0:T(8,128)(2,1)S(1)} %all-to-all-done.1), channel_id=1, source_target_pairs={{0,0},{1,256},{256,1},{257,257},{2,2},{3,258},{258,3},{259,259},{4... | collective-permute-start | bytes 393224 | tf_op jit(solution)/shard_map/ppermute | solution.py:102
  45.7 3.6 %shard_map.37 = (bf16[1024,512]{1,0:T(8,128)(2,1)S(1)}, bf16[512,512]{1,0:T(8,128)(2,1)}, bf16[512,1024]{1,0:T(8,128)(2,1)S(1)}, f32[256,256]{1,0:T(8,128)}, f32...) custom-call(), custom_call_target="tpu_custom_call" | custom-call | tf_op jit(solution)/shard_map/pallas_call | solution.py:106
  49.3 0.0 copy-start.1
  49.3 0.7 copy-done.1
  49.9 0.6 dynamic_slice.3.gain
  50.6 3.3 %collective-permute-done = bf16[32,8,256]{2,1,0:T(8,128)(2,1)S(1)} collective-permute-done((bf16[32,8,256]{2,1,0:T(8,128)(2,1)S(1)}, bf16[32,8,256]{2,1,0:T(8,128)(2,1)S(1)}, u32[]{:S(2)}, u32[]{:S(2)}) %collective-permute-start) | collective-permute-done | bytes 131104 | tf_op jit(solution)/shard_map/ppermute | solution.py:102
  53.8 2.0 %all_gather.3 = bf16[64,8,256]{2,1,0:T(8,128)(2,1)S(1)} all-gather(bf16[32,8,256]{2,1,0:T(8,128)(2,1)S(1)} %collective-permute-done), channel_id=1, replica_groups=mesh['yh'=2,'xz'=32,'ylo'=4,'core'=2] {'core'}, dimensions={0}, use_global_device_ids=true | all-gather | bytes 393216 | tf_op jit(solution)/shard_map/all_gather | solution.py:103
  55.8 0.3 all-to-all-done
  56.1 6.3 %shard_map.38 = bf16[4,512,128]{2,1,0:T(8,128)(2,1)S(1)} custom-call(f32[1]{0:T(128)} %dynamic_slice.3.gain, bf16[4,512,128]{2,1,0:T(8,128)(2,1)S(1)} %bitcast.10, bf16[512,256]{1,0:T(8,128)(2,1)S(1)} %bitcast.12, bf16[1024,512]{1,0:T(8,128)(2,1)S(1)} %get-tuple-element.11.first, bf16[512,1024]{1,0:T(8,128)(2,1)S(1)} %get-tuple-element.12.fourth, ...), custom_call_target="tpu_custom_call" | custom-call | tf_op jit(solution)/shard_map/pallas_call | solution.py:122
  62.4 34.7 %all_to_all.15 = bf16[256,8,128]{2,1,0:T(8,128)(2,1)S(1)} all-to-all(bf16[256,8,128]{2,1,0:T(8,128)(2,1)S(1)} %bitcast.11), channel_id=1, replica_groups=mesh['yh'=2,'xz'=32,'ylo'=4,'core'=2] {'ylo','yh','xz'}, dimensions={0} | all-to-all | bytes 1048576 | tf_op jit(solution)/shard_map/all_to_all | solution.py:137
  97.0 1.1 %copy.9 = bf16[8,128,256]{2,1,0:T(8,128)(2,1)} copy(bf16[8,128,256]{1,0,2:T(8,128)(2,1)S(1)} %bitcast.13) | data formatting | bytes 1048576 | tf_op jit(solution)/shard_map/transpose | solution.py:138
Async XLA Ops:
  0.0 15.4 %copy-start = (bf16[1,1024,256]{2,1,0:T(8,128)(2,1)S(1)}, bf16[1,1024,256]{2,1,0:T(8,128)(2,1)}, u32[]{:S(2)}) copy-start(bf16[1,1024,256]{2,1,0:T(8,128)(2,1)} %param.3) | copy-start | bytes 1572868
  1.7 22.9 %all-to-all-start.1 = ((bf16[32,8,256]{2,1,0:T(8,128)(2,1)}), bf16[32,8,256]{2,1,0:T(8,128)(2,1)S(1)}, u32[]{:S(2)}, u32[]{:S(2)}) async-start(bf16[32,8,256]{2,1,0:T(8,128)(2,1)} %copy.10), calls=%async_computation.1 | async-start | bytes 262144 | tf_op jit(solution)/shard_map/all_to_all | solution.py:101
  24.6 31.5 %all-to-all-start = ((bf16[256,8,128]{2,1,0:T(8,128)(2,1)}), bf16[256,8,128]{2,1,0:T(8,128)(2,1)S(1)}, u32[]{:S(2)}, u32[]{:S(2)}) async-start(bf16[256,8,128]{2,1,0:T(8,128)(2,1)} %bitcast.1), calls=%async_computation | async-start | bytes 1048576 | tf_op jit(solution)/shard_map/all_to_all | solution.py:98
  37.8 16.1 %collective-permute-start = (bf16[32,8,256]{2,1,0:T(8,128)(2,1)S(1)}, bf16[32,8,256]{2,1,0:T(8,128)(2,1)S(1)}, u32[]{:S(2)}, u32[]{:S(2)}) collective-permute-start(bf16[32,8,256]{2,1,0:T(8,128)(2,1)S(1)} %all-to-all-done.1), channel_id=1, source_target_pairs={{0,0},{1,256},{256,1},{257,257},{2,2},{3,258},{258,3},{259,259},{4... | collective-permute-start | bytes 393224 | tf_op jit(solution)/shard_map/ppermute | solution.py:102
  49.3 0.7 copy-start.1

commit v4 on v3

v4 whole, which is shorter than its diff:
```python
import math

import jax
import jax.numpy as jnp
import numpy as np
from jax import lax
from jax.experimental import pallas as pl
from jax.experimental.pallas import tpu as pltpu
from jax.sharding import Mesh
from jax.sharding import PartitionSpec as P


N1 = 256
N2 = 256
HALF = 128
EVERY = ("yh", "xz", "ylo", "core")


def home(ylo, core):
    return (ylo + 2 + 4 * core) % 8


TOKEN_GROUPS = [
    [
        ((home(ylo, block) // 4 * 32 + xz) * 4 + home(ylo, block) % 4) * 2 + core
        for ylo in range(4)
        for block in range(2)
        for xz in range(32)
    ]
    for core in range(2)
]
MEET = [
    ((yh * 4 + ylo) * 2 + core, home(ylo, core) * 2 + yh)
    for yh in range(2)
    for ylo in range(4)
    for core in range(2)
]
VMEM = pl.BlockSpec(memory_space=pltpu.VMEM)
HBM = pl.BlockSpec(memory_space=pltpu.HBM)
KERNEL = pltpu.CompilerParams(vmem_limit_bytes=24 * 1024 * 1024)


def grid_of(shape, dim):
    return lax.broadcasted_iota(jnp.int32, shape, dim)


def cos_sin(period):
    steps = np.arange(N1)
    angle = (steps[:, None] * steps[None, :] % period) * (2.0 * math.pi / period)
    return np.cos(angle).astype(np.float32), np.sin(angle).astype(np.float32)


def complex_table():
    c, s = cos_sin(N2)
    return np.block([[c, -s], [s, c]]).astype(jnp.bfloat16)


def make_tables(second, first, fourth, order):
    c16, n16 = second[:N2, :N2], second[:N2, N2:]
    tall, wide = jnp.concatenate([c16, n16], axis=0), jnp.concatenate([c16, n16], axis=1)
    for half in range(2):
        spread = (N1, 2 * N1)
        pick = jnp.where(grid_of(spread, 1) == 2 * grid_of(spread, 0) + half, 1.0, 0.0).astype(jnp.bfloat16)
        block = dot(tall, pick).astype(jnp.bfloat16)
        first[half * N1 : (half + 1) * N1, :] = block[:N1]
        first[(2 + half) * N1 : (3 + half) * N1, :] = block[N1:]
        spread = (2 * N1, N1)
        pick = jnp.where(grid_of(spread, 0) == 2 * grid_of(spread, 1) + half, 1.0, 0.0).astype(jnp.bfloat16)
        block = dot(pick, wide).astype(jnp.bfloat16)
        fourth[:, half * N1 : (half + 1) * N1] = block[:, :N1]
        fourth[:, (2 + half) * N1 : (3 + half) * N1] = block[:, N1:]
    full = (HALF, HALF)
    want = grid_of(full, 0)
    source = (want // 4 % 16) * 8 + (want // 64) * 4 + want % 4
    order[...] = jnp.where(source == grid_of(full, 1), 1.0, 0.0).astype(jnp.bfloat16)


def dot(a, b):
    return jnp.dot(a, b, preferred_element_type=jnp.float32)


def convolve(gains_hbm, u, filt, order, first, second, cos_tw, sin_tw, fourth_hbm, out, gains, fourth, arrived):
    copies = (
        pltpu.make_async_copy(gains_hbm, gains, arrived.at[0]),
        pltpu.make_async_copy(fourth_hbm, fourth, arrived.at[1]),
    )
    for copy in copies:
        copy.start()
    block = (lax.axis_index("yh") * 4 + lax.axis_index("ylo") + 6) % 8
    channel = (block % 4) * 64 + (block // 4) * 32 + lax.axis_index("xz")
    batches = u.shape[0]
    section = dot(first[...], jnp.concatenate([u[b] for b in range(batches)], axis=1))
    blocks = [dot(order[...], filt[i * HALF : (i + 1) * HALF]) for i in range(4)]
    wr = jnp.concatenate([block[:64] for block in blocks], axis=0)
    wi = jnp.concatenate([block[64:] for block in blocks], axis=0)
    c, s = cos_tw[...], sin_tw[...]
    for first_of_two in range(0, batches, 2):
        two = []
        for b in (first_of_two, first_of_two + 1):
            piece = section[:, b * HALF : (b + 1) * HALF]
            re = jnp.concatenate([piece[:N1], piece[N1 : 2 * N1]], axis=1)
            im = jnp.concatenate([piece[2 * N1 : 3 * N1], piece[3 * N1 :]], axis=1)
            turned = jnp.concatenate([re * c + im * s, im * c - re * s], axis=1).astype(jnp.bfloat16)
            spectrum = dot(turned, second[...])
            sr, si = spectrum[:, :N2], spectrum[:, N2:]
            product = jnp.concatenate([sr * wr - si * wi, -(sr * wi) - si * wr], axis=1).astype(jnp.bfloat16)
            back = dot(product, second[...])
            br, nbi = back[:, :N2], back[:, N2:]
            tr = (br * c + nbi * s).astype(jnp.bfloat16)
            ti = (br * s - nbi * c).astype(jnp.bfloat16)
            two.append(jnp.concatenate([tr[:, :HALF], tr[:, HALF:], ti[:, :HALF], ti[:, HALF:]], axis=0))
        if first_of_two == 0:
            for copy in copies:
                copy.wait()
        filtered = dot(fourth[...], jnp.concatenate(two, axis=1)) * (1.0 / (N1 * N2))
        for i in range(2):
            b = first_of_two + i
            skip = gains[channel] * u[b].astype(jnp.float32)
            out[b] = (filtered[:, i * HALF : (i + 1) * HALF] + skip).astype(jnp.bfloat16)


def exchange(chunks):
    return lax.all_to_all(
        chunks, EVERY, split_axis=0, concat_axis=0, tiled=True, axis_index_groups=TOKEN_GROUPS
    )


def layer(tokens, filter_spectrum, skip_gain):
    channels = tokens.shape[-1]
    mine = filter_spectrum.transpose(3, 0, 1, 2).reshape(32, 8, N2)
    mine = lax.all_to_all(mine, "xz", split_axis=0, concat_axis=0, tiled=True)
    laid_out = tokens.reshape(8, HALF, channels).transpose(2, 0, 1)
    u = exchange(laid_out)
    u = u.reshape(4, 2 * N1, HALF)
    mine = lax.ppermute(mine, ("yh", "ylo", "core"), MEET)
    filt = lax.all_gather(mine, "core", axis=0, tiled=True)
    filt = filt.reshape(2 * N1, N2)
    second = jnp.asarray(complex_table())
    cos_tw, sin_tw = (jnp.asarray(table) for table in cos_sin(N1 * N2))
    first, fourth, order = pl.pallas_call(
        make_tables,
        out_shape=[
            jax.ShapeDtypeStruct((4 * N1, 2 * N1), jnp.bfloat16),
            pltpu.HBM((2 * N1, 4 * N1), jnp.bfloat16),
            jax.ShapeDtypeStruct((HALF, HALF), jnp.bfloat16),
        ],
        in_specs=[VMEM],
        out_specs=[VMEM, VMEM, VMEM],
        compiler_params=KERNEL,
    )(second)
    fourth = pltpu.with_memory_space_constraint(fourth, pltpu.HBM)
    gains = pltpu.with_memory_space_constraint(skip_gain, pltpu.HBM)
    mixed = pl.pallas_call(
        convolve,
        out_shape=jax.ShapeDtypeStruct((4, 2 * N1, HALF), jnp.bfloat16),
        in_specs=[HBM] + [VMEM] * 7 + [HBM],
        out_specs=VMEM,
        scratch_shapes=[
            pltpu.SMEM((N1,), jnp.float32),
            pltpu.VMEM((2 * N1, 4 * N1), jnp.bfloat16),
            pltpu.SemaphoreType.DMA((2,)),
        ],
        compiler_params=KERNEL,
    )(gains, u, filt, order, first, second, cos_tw, sin_tw, fourth)
    mixed = mixed.reshape(4 * 64, 8, HALF)
    back = exchange(mixed)
    return back.transpose(1, 2, 0).reshape(1, 8 * HALF, channels)


def solution(mesh):
    split = Mesh(mesh.devices.reshape(2, 32, 4, 2), ("yh", "xz", "ylo", "core"))
    bat, seq = ("ylo", "core"), ("yh", "xz")
    placed = (P(bat, seq, None), P(None, seq, None, bat), P())
    return jax.shard_map(layer, mesh=split, in_specs=placed, out_specs=P(bat, seq, None), check_vma=False)
```

time: 98.5 us -> 94.9 us (0.963)
  Pallas kernels: 9.83 us -> 5.39 us
  waiting for transfers between devices: 11.6 us -> 14.6 us
  starting transfers between devices: 34.8 us -> 33.4 us
  local copies, waits for them, and re-layouts: 5.18 us -> 3.9 us
    pallas_call x1, Pallas kernels: 6.26 us -> 3.66 us  [layer(): pl.pallas_call(convolve, out_shape=jax.ShapeDtypeStruct((4, 2 * N1, HALF)...]
    ppermute x1, waiting for transfers between devices: 3.29 us -> 5.78 us  [layer(): mine = lax.ppermute(mine, ('yh', 'ylo', 'core'), MEET)]
    pallas_call x1, Pallas kernels: 3.57 us -> 1.73 us  [layer(): pl.pallas_call(make_tables, out_shape=[jax.ShapeDtypeStruct((4 * N1, 2 *...]
    ppermute x1, starting transfers between devices: 7.9 us -> 6.61 us  [layer(): mine = lax.ppermute(mine, ('yh', 'ylo', 'core'), MEET)]
  transfers between devices with their start and end apart: 3 -> 3, of which waited for: 3 -> 3; matrix products, arithmetic and copies ran while one was open for 2% -> 1% of each run, Pallas kernels for 4% -> 2%
where the time goes in v4:
time: 94.9 us; the launch traced here: 94.1 us
  blocking collectives  36.7 us (39%)
  starting transfers between devices  33.4 us (35%)
  waiting for transfers between devices  14.6 us (15%)
  Pallas kernels  5.39 us (6%)
  local copies, waits for them, and re-layouts  3.9 us (4%)
    all_to_all x1, blocking collectives, exchange(): lax.all_to_all(chunks, EVERY, split_axis=0, concat_axis=0, tiled=True, ax...  34.7 us
    all_to_all x1, starting transfers between devices, layer(): mine = lax.all_to_all(mine, 'xz', split_axis=0, concat_axis=0, tiled=True)  13.7 us
    all_to_all x1, starting transfers between devices, exchange(): lax.all_to_all(chunks, EVERY, split_axis=0, concat_axis=0, tiled=True, ax...  13.1 us
    all_to_all x1, waiting for transfers between devices, layer(): mine = lax.all_to_all(mine, 'xz', split_axis=0, concat_axis=0, tiled=True)  8.07 us
    ppermute x1, starting transfers between devices, layer(): mine = lax.ppermute(mine, ('yh', 'ylo', 'core'), MEET)  6.61 us
    ppermute x1, waiting for transfers between devices, layer(): mine = lax.ppermute(mine, ('yh', 'ylo', 'core'), MEET)  5.78 us
    pallas_call x1, Pallas kernels, layer(): pl.pallas_call(convolve, out_shape=jax.ShapeDtypeStruct((4, 2 * N1, HALF)...  3.66 us
    all_gather x1, blocking collectives, layer(): filt = lax.all_gather(mine, 'core', axis=0, tiled=True)  1.98 us
  transfers between devices with their start and end apart: 3, of which 3 were waited for; matrix products, arithmetic and copies ran while one was open for 1% of the time, Pallas kernels for 2%

profile of v4, /device:TPU:1, one launch (start us, length us, event | category | flops | bytes accessed | tf_op | source)
XLA Modules:
  0.0 94.1 jit_solution(8493426577179267944)
XLA Ops:
  0.0 0.0 copy-start.3
  0.0 1.7 %copy.13 = bf16[32,8,256]{2,1,0:T(8,128)(2,1)} copy(bf16[32,8,256]{2,0,1:T(8,128)(2,1)} %bitcast.15) | data formatting | bytes 262144 | tf_op jit(solution)/shard_map/reshape | solution.py:130
  1.7 13.7 %all-to-all-start.1 = ((bf16[32,8,256]{2,1,0:T(8,128)(2,1)}), bf16[32,8,256]{2,1,0:T(8,128)(2,1)S(1)}, u32[]{:S(2)}, u32[]{:S(2)}) async-start(bf16[32,8,256]{2,1,0:T(8,128)(2,1)} %copy.13), calls=%async_computation.1 | async-start | bytes 262144 | tf_op jit(solution)/shard_map/all_to_all | solution.py:131
  15.4 0.0 copy-done.3
  15.4 1.1 %copy.10 = bf16[8,128,256]{1,0,2:T(8,128)(2,1)} copy(bf16[8,128,256]{2,1,0:T(8,128)(2,1)S(1)} %bitcast.14) | data formatting | bytes 1048576 | tf_op jit(solution)/shard_map/reshape | solution.py:132
  16.5 8.1 %all-to-all-done.1 = bf16[32,8,256]{2,1,0:T(8,128)(2,1)S(1)} async-done(((bf16[32,8,256]{2,1,0:T(8,128)(2,1)}), bf16[32,8,256]{2,1,0:T(8,128)(2,1)S(1)}, u32[]{:S(2)}, u32[]{:S(2)}) %all-to-all-start.1) | async-done | bytes 131104 | tf_op jit(solution)/shard_map/all_to_all | solution.py:131
  24.6 0.0 copy-start
  24.6 13.1 %all-to-all-start = ((bf16[256,8,128]{2,1,0:T(8,128)(2,1)}), bf16[256,8,128]{2,1,0:T(8,128)(2,1)S(1)}, u32[]{:S(2)}, u32[]{:S(2)}) async-start(bf16[256,8,128]{2,1,0:T(8,128)(2,1)} %bitcast.1), calls=%async_computation | async-start | bytes 1048576 | tf_op jit(solution)/shard_map/all_to_all | solution.py:123
  37.6 6.6 %collective-permute-start = (bf16[32,8,256]{2,1,0:T(8,128)(2,1)S(1)}, bf16[32,8,256]{2,1,0:T(8,128)(2,1)S(1)}, u32[]{:S(2)}, u32[]{:S(2)}) collective-permute-start(bf16[32,8,256]{2,1,0:T(8,128)(2,1)S(1)} %all-to-all-done.1), channel_id=1, source_target_pairs={{0,4},{1,260},{2,6},{3,262},{4,256},{5,0},{6,258},{7,2},{256,5},{2... | collective-permute-start | bytes 393224 | tf_op jit(solution)/shard_map/ppermute | solution.py:135
  44.2 0.0 copy-done
  44.3 0.0 copy-start.2
  44.3 1.7 %shard_map.64 = (bf16[1024,512]{1,0:T(8,128)(2,1)S(1)}, bf16[512,1024]{1,0:T(8,128)(2,1)}, bf16[128,128]{1,0:T(8,128)(2,1)S(1)}) custom-call(bf16[512,512]{1,0:T(8,128)(2,1)S(1)} %copy-done), custom_call_target="tpu_custom_call" | custom-call | tf_op jit(solution)/shard_map/pallas_call | solution.py:140
  46.0 0.0 copy-start.1
  46.0 5.8 %collective-permute-done = bf16[32,8,256]{2,1,0:T(8,128)(2,1)S(1)} collective-permute-done((bf16[32,8,256]{2,1,0:T(8,128)(2,1)S(1)}, bf16[32,8,256]{2,1,0:T(8,128)(2,1)S(1)}, u32[]{:S(2)}, u32[]{:S(2)}) %collective-permute-start) | collective-permute-done | bytes 131104 | tf_op jit(solution)/shard_map/ppermute | solution.py:135
  51.8 2.0 %all_gather.3 = bf16[64,8,256]{2,1,0:T(8,128)(2,1)S(1)} all-gather(bf16[32,8,256]{2,1,0:T(8,128)(2,1)S(1)} %collective-permute-done), channel_id=1, replica_groups=mesh['yh'=2,'xz'=32,'ylo'=4,'core'=2] {'core'}, dimensions={0}, use_global_device_ids=true | all-gather | bytes 393216 | tf_op jit(solution)/shard_map/all_gather | solution.py:136
  53.8 0.8 all-to-all-done
  54.5 0.0 copy-done.2
  54.5 0.0 copy-done.1
  54.5 3.7 %shard_map.65 = bf16[4,512,128]{2,1,0:T(8,128)(2,1)S(1)} custom-call(f32[256]{0:T(256)} %gains_hbm.1, bf16[4,512,128]{2,1,0:T(8,128)(2,1)S(1)} %bitcast.10, bf16[512,256]{1,0:T(8,128)(2,1)S(1)} %bitcast.12, bf16[128,128]{1,0:T(8,128)(2,1)S(1)} %get-tuple-element.8.order, bf16[1024,512]{1,0:T(8,128)(2,1)S(1)} %get-tuple-element.9.first, ...), custom_call_target="tpu_custom_call" | custom-call | tf_op jit(solution)/shard_map/pallas_call | solution.py:153
  58.2 34.7 %all_to_all.15 = bf16[256,8,128]{2,1,0:T(8,128)(2,1)S(1)} all-to-all(bf16[256,8,128]{2,1,0:T(8,128)(2,1)S(1)} %bitcast.11), channel_id=1, replica_groups={{4,12,20,28,36,44,52,60,68,76,84,92,100,108,116,124,132,140,148,156,164..., dimensions={0} | all-to-all | bytes 1048576 | tf_op jit(solution)/shard_map/all_to_all | solution.py:123
  93.0 1.1 %copy.12 = bf16[8,128,256]{2,1,0:T(8,128)(2,1)} copy(bf16[8,128,256]{1,0,2:T(8,128)(2,1)S(1)} %bitcast.13) | data formatting | bytes 1048576 | tf_op jit(solution)/shard_map/transpose | solution.py:167
Async XLA Ops:
  0.0 15.4 %copy-start.3 = (bf16[1,1024,256]{2,1,0:T(8,128)(2,1)S(1)}, bf16[1,1024,256]{2,1,0:T(8,128)(2,1)}, u32[]{:S(2)}) copy-start(bf16[1,1024,256]{2,1,0:T(8,128)(2,1)} %param.6) | copy-start | bytes 1572868
  1.7 22.9 %all-to-all-start.1 = ((bf16[32,8,256]{2,1,0:T(8,128)(2,1)}), bf16[32,8,256]{2,1,0:T(8,128)(2,1)S(1)}, u32[]{:S(2)}, u32[]{:S(2)}) async-start(bf16[32,8,256]{2,1,0:T(8,128)(2,1)} %copy.13), calls=%async_computation.1 | async-start | bytes 262144 | tf_op jit(solution)/shard_map/all_to_all | solution.py:131
  24.6 19.7 %copy-start = (bf16[512,512]{1,0:T(8,128)(2,1)S(1)}, bf16[512,512]{1,0:T(8,128)(2,1)}, u32[]{:S(2)}) copy-start(bf16[512,512]{1,0:T(8,128)(2,1)} %constant.6.clone.second) | copy-start | bytes 1572868
  24.6 30.0 %all-to-all-start = ((bf16[256,8,128]{2,1,0:T(8,128)(2,1)}), bf16[256,8,128]{2,1,0:T(8,128)(2,1)S(1)}, u32[]{:S(2)}, u32[]{:S(2)}) async-start(bf16[256,8,128]{2,1,0:T(8,128)(2,1)} %bitcast.1), calls=%async_computation | async-start | bytes 1048576 | tf_op jit(solution)/shard_map/all_to_all | solution.py:123
  37.6 14.2 %collective-permute-start = (bf16[32,8,256]{2,1,0:T(8,128)(2,1)S(1)}, bf16[32,8,256]{2,1,0:T(8,128)(2,1)S(1)}, u32[]{:S(2)}, u32[]{:S(2)}) collective-permute-start(bf16[32,8,256]{2,1,0:T(8,128)(2,1)S(1)} %all-to-all-done.1), channel_id=1, source_target_pairs={{0,4},{1,260},{2,6},{3,262},{4,256},{5,0},{6,258},{7,2},{256,5},{2... | collective-permute-start | bytes 393224 | tf_op jit(solution)/shard_map/ppermute | solution.py:135
  44.3 10.3 %copy-start.2 = (f32[256,256]{1,0:T(8,128)S(1)}, f32[256,256]{1,0:T(8,128)}, u32[]{:S(2)}) copy-start(f32[256,256]{1,0:T(8,128)} %constant.7.clone.cos_tw) | copy-start | bytes 786436
  46.0 8.5 %copy-start.1 = (f32[256,256]{1,0:T(8,128)S(1)}, f32[256,256]{1,0:T(8,128)}, u32[]{:S(2)}) copy-start(f32[256,256]{1,0:T(8,128)} %constant.8.clone.sin_tw) | copy-start | bytes 786436

commit v5 on v4

v5 whole, which is shorter than its diff:
```python
import math

import jax
import jax.numpy as jnp
import numpy as np
from jax import lax
from jax.experimental import pallas as pl
from jax.experimental.pallas import tpu as pltpu
from jax.sharding import Mesh
from jax.sharding import PartitionSpec as P


N1 = 256
N2 = 256
HALF = 128
ROWS = 512
EVERY = ("yh", "xz", "ylo", "core")


def home(ylo, core):
    return (ylo + 2 + 4 * core) % 8


TOKEN_GROUPS = [
    [
        ((home(ylo, block) // 4 * 32 + xz) * 4 + home(ylo, block) % 4) * 2 + core
        for ylo in range(4)
        for block in range(2)
        for xz in range(32)
    ]
    for core in range(2)
]
MEET = [
    ((yh * 4 + ylo) * 2 + core, home(ylo, core) * 2 + yh)
    for yh in range(2)
    for ylo in range(4)
    for core in range(2)
]
VMEM = pl.BlockSpec(memory_space=pltpu.VMEM)
HBM = pl.BlockSpec(memory_space=pltpu.HBM)
KERNEL = pltpu.CompilerParams(vmem_limit_bytes=24 * 1024 * 1024)


def cos_sin(rows, columns, period):
    angle = (np.arange(rows)[:, None] * np.arange(columns)[None, :] % period) * (2.0 * math.pi / period)
    return np.cos(angle).astype(np.float32), np.sin(angle).astype(np.float32)


def tables():
    c, s = cos_sin(ROWS, ROWS, ROWS)
    ch, sh = cos_sin(HALF, HALF, HALF)
    inner = np.block([[ch, -sh], [sh, ch]])
    want = np.arange(HALF)
    source = (want // 4 % 16) * 8 + (want // 64) * 4 + want % 4
    order = source[:, None] == np.arange(HALF)[None, :]
    want = np.arange(N2)
    parity = np.arange(N2)[:, None] == (want % HALF * 2 + want // HALF)[None, :]
    half = [np.asarray(table, np.float32).astype(jnp.bfloat16) for table in (c, -s, inner, order, parity)]
    return [jnp.asarray(table) for table in (*half, *cos_sin(ROWS, HALF, N1 * N2))]


def dot(a, b):
    return jnp.dot(a, b, preferred_element_type=jnp.float32)


def convolve(gains_hbm, u, filt, cos_rows, sin_rows, inner, order, parity, cos_tw, sin_tw, out, gains, arrived):
    copy = pltpu.make_async_copy(gains_hbm, gains, arrived)
    copy.start()
    block = (lax.axis_index("yh") * 4 + lax.axis_index("ylo") + 6) % 8
    channel = (block % 4) * 64 + (block // 4) * 32 + lax.axis_index("xz")
    batches = u.shape[0]
    wide = jnp.concatenate([u[b] for b in range(batches)], axis=1)
    section_re, section_im = dot(cos_rows[...], wide), dot(sin_rows[...], wide)
    blocks = [dot(order[...], filt[i * HALF : (i + 1) * HALF]).astype(jnp.bfloat16) for i in range(4)]
    parts = [block[:64] for block in blocks] + [block[64:] for block in blocks]
    weights = dot(jnp.concatenate(parts, axis=0), parity[...])
    wr = jnp.concatenate([weights[:N1, :HALF], weights[:N1, HALF:]], axis=0)
    wi = jnp.concatenate([weights[N1:, :HALF], weights[N1:, HALF:]], axis=0)
    c, s = cos_tw[...], sin_tw[...]
    for first_of_two in range(0, batches, 2):
        rows_re, rows_im = [], []
        for b in (first_of_two, first_of_two + 1):
            re, im = section_re[:, b * HALF : (b + 1) * HALF], section_im[:, b * HALF : (b + 1) * HALF]
            turned = jnp.concatenate([re * c + im * s, im * c - re * s], axis=1).astype(jnp.bfloat16)
            spectrum = dot(turned, inner[...])
            sr, si = spectrum[:, :HALF], spectrum[:, HALF:]
            product = jnp.concatenate([sr * wr - si * wi, -(sr * wi) - si * wr], axis=1).astype(jnp.bfloat16)
            back = dot(product, inner[...])
            br, nbi = back[:, :HALF], back[:, HALF:]
            rows_re.append((br * c + nbi * s).astype(jnp.bfloat16))
            rows_im.append((br * s - nbi * c).astype(jnp.bfloat16))
        if first_of_two == 0:
            copy.wait()
        filtered = dot(cos_rows[...], jnp.concatenate(rows_re, axis=1))
        filtered = filtered + dot(sin_rows[...], jnp.concatenate(rows_im, axis=1))
        filtered = filtered * (1.0 / (N1 * N2))
        for i in range(2):
            b = first_of_two + i
            skip = gains[channel] * u[b].astype(jnp.float32)
            out[b] = (filtered[:, i * HALF : (i + 1) * HALF] + skip).astype(jnp.bfloat16)


def exchange(chunks):
    return lax.all_to_all(
        chunks, EVERY, split_axis=0, concat_axis=0, tiled=True, axis_index_groups=TOKEN_GROUPS
    )


def layer(tokens, filter_spectrum, skip_gain):
    channels = tokens.shape[-1]
    mine = filter_spectrum.transpose(3, 0, 1, 2).reshape(32, 8, N2)
    mine = lax.all_to_all(mine, "xz", split_axis=0, concat_axis=0, tiled=True)
    laid_out = tokens.reshape(8, HALF, channels).transpose(2, 0, 1)
    u = exchange(laid_out)
    u = u.reshape(4, ROWS, HALF)
    mine = lax.ppermute(mine, ("yh", "ylo", "core"), MEET)
    filt = lax.all_gather(mine, "core", axis=0, tiled=True)
    filt = filt.reshape(ROWS, N2)
    gains = pltpu.with_memory_space_constraint(skip_gain, pltpu.HBM)
    mixed = pl.pallas_call(
        convolve,
        out_shape=jax.ShapeDtypeStruct((4, ROWS, HALF), jnp.bfloat16),
        in_specs=[HBM] + [VMEM] * 9,
        out_specs=VMEM,
        scratch_shapes=[pltpu.SMEM((N1,), jnp.float32), pltpu.SemaphoreType.DMA],
        compiler_params=KERNEL,
    )(gains, u, filt, *tables())
    mixed = mixed.reshape(4 * 64, 8, HALF)
    back = exchange(mixed)
    return back.transpose(1, 2, 0).reshape(1, 8 * HALF, channels)


def solution(mesh):
    split = Mesh(mesh.devices.reshape(2, 32, 4, 2), ("yh", "xz", "ylo", "core"))
    bat, seq = ("ylo", "core"), ("yh", "xz")
    placed = (P(bat, seq, None), P(None, seq, None, bat), P())
    return jax.shard_map(layer, mesh=split, in_specs=placed, out_specs=P(bat, seq, None), check_vma=False)
```

time: 94.9 us -> 94.1 us (level)
  Pallas kernels: 5.39 us -> 2.87 us
  waiting for transfers between devices: 14.6 us -> 16 us
    pallas_call x2 -> x1, Pallas kernels: 5.39 us -> 2.87 us  [layer(): pl.pallas_call(convolve, out_shape=jax.ShapeDtypeStruct((4, ROWS, HALF),...]
    ppermute x1, waiting for transfers between devices: 5.78 us -> 7.38 us  [layer(): mine = lax.ppermute(mine, ('yh', 'ylo', 'core'), MEET)]
  transfers between devices with their start and end apart: 3 -> 3, of which waited for: 3 -> 3; matrix products, arithmetic and copies ran while one was open for 1% -> 1% of each run, Pallas kernels for 2% -> 0%
where the time goes in v5:
time: 94.1 us; the launch traced here: 93.3 us
  blocking collectives  36.9 us (39%)
  starting transfers between devices  33.5 us (36%)
  waiting for transfers between devices  16 us (17%)
  local copies, waits for them, and re-layouts  3.93 us (4%)
  Pallas kernels  2.87 us (3%)
    all_to_all x1, blocking collectives, exchange(): lax.all_to_all(chunks, EVERY, split_axis=0, concat_axis=0, tiled=True, ax...  34.9 us
    all_to_all x1, starting transfers between devices, layer(): mine = lax.all_to_all(mine, 'xz', split_axis=0, concat_axis=0, tiled=True)  13.7 us
    all_to_all x1, starting transfers between devices, exchange(): lax.all_to_all(chunks, EVERY, split_axis=0, concat_axis=0, tiled=True, ax...  13.1 us
    all_to_all x1, waiting for transfers between devices, layer(): mine = lax.all_to_all(mine, 'xz', split_axis=0, concat_axis=0, tiled=True)  8.03 us
    ppermute x1, waiting for transfers between devices, layer(): mine = lax.ppermute(mine, ('yh', 'ylo', 'core'), MEET)  7.38 us
    ppermute x1, starting transfers between devices, layer(): mine = lax.ppermute(mine, ('yh', 'ylo', 'core'), MEET)  6.75 us
    pallas_call x1, Pallas kernels, layer(): pl.pallas_call(convolve, out_shape=jax.ShapeDtypeStruct((4, ROWS, HALF),...  2.87 us
    all_gather x1, blocking collectives, layer(): filt = lax.all_gather(mine, 'core', axis=0, tiled=True)  1.98 us
  transfers between devices with their start and end apart: 3, of which 3 were waited for; matrix products, arithmetic and copies ran while one was open for 1% of the time, Pallas kernels for 0%

profile of v5, /device:TPU:1, one launch (start us, length us, event | category | flops | bytes accessed | tf_op | source)
XLA Modules:
  0.0 93.3 jit_solution(6119396120446890523)
XLA Ops:
  0.0 0.0 copy-start.7
  0.0 1.7 %copy.17 = bf16[32,8,256]{2,1,0:T(8,128)(2,1)} copy(bf16[32,8,256]{2,0,1:T(8,128)(2,1)} %bitcast.15) | data formatting | bytes 262144 | tf_op jit(solution)/shard_map/reshape | solution.py:111
  1.7 13.7 %all-to-all-start.1 = ((bf16[32,8,256]{2,1,0:T(8,128)(2,1)}), bf16[32,8,256]{2,1,0:T(8,128)(2,1)S(1)}, u32[]{:S(2)}, u32[]{:S(2)}) async-start(bf16[32,8,256]{2,1,0:T(8,128)(2,1)} %copy.17), calls=%async_computation.1 | async-start | bytes 262144 | tf_op jit(solution)/shard_map/all_to_all | solution.py:112
  15.4 0.0 copy-done.7
  15.4 0.0 copy-start.3
  15.4 0.0 copy-start.5
  15.4 0.0 copy-start.6
  15.5 1.1 %copy.14 = bf16[8,128,256]{1,0,2:T(8,128)(2,1)} copy(bf16[8,128,256]{2,1,0:T(8,128)(2,1)S(1)} %bitcast.14) | data formatting | bytes 1048576 | tf_op jit(solution)/shard_map/reshape | solution.py:113
  16.5 8.0 %all-to-all-done.1 = bf16[32,8,256]{2,1,0:T(8,128)(2,1)S(1)} async-done(((bf16[32,8,256]{2,1,0:T(8,128)(2,1)}), bf16[32,8,256]{2,1,0:T(8,128)(2,1)S(1)}, u32[]{:S(2)}, u32[]{:S(2)}) %all-to-all-start.1) | async-done | bytes 131104 | tf_op jit(solution)/shard_map/all_to_all | solution.py:112
  24.6 0.0 copy-start
  24.6 0.0 copy-start.1
  24.6 13.1 %all-to-all-start = ((bf16[256,8,128]{2,1,0:T(8,128)(2,1)}), bf16[256,8,128]{2,1,0:T(8,128)(2,1)S(1)}, u32[]{:S(2)}, u32[]{:S(2)}) async-start(bf16[256,8,128]{2,1,0:T(8,128)(2,1)} %bitcast.1), calls=%async_computation | async-start | bytes 1048576 | tf_op jit(solution)/shard_map/all_to_all | solution.py:104
  37.6 0.0 copy-start.2
  37.6 0.0 copy-start.4
  37.7 6.7 %collective-permute-start = (bf16[32,8,256]{2,1,0:T(8,128)(2,1)S(1)}, bf16[32,8,256]{2,1,0:T(8,128)(2,1)S(1)}, u32[]{:S(2)}, u32[]{:S(2)}) collective-permute-start(bf16[32,8,256]{2,1,0:T(8,128)(2,1)S(1)} %all-to-all-done.1), channel_id=1, source_target_pairs={{0,4},{1,260},{2,6},{3,262},{4,256},{5,0},{6,258},{7,2},{256,5},{2... | collective-permute-start | bytes 393224 | tf_op jit(solution)/shard_map/ppermute | solution.py:116
  44.4 7.4 %collective-permute-done = bf16[32,8,256]{2,1,0:T(8,128)(2,1)S(1)} collective-permute-done((bf16[32,8,256]{2,1,0:T(8,128)(2,1)S(1)}, bf16[32,8,256]{2,1,0:T(8,128)(2,1)S(1)}, u32[]{:S(2)}, u32[]{:S(2)}) %collective-permute-start) | collective-permute-done | bytes 131104 | tf_op jit(solution)/shard_map/ppermute | solution.py:116
  51.8 2.0 %all_gather.3 = bf16[64,8,256]{2,1,0:T(8,128)(2,1)S(1)} all-gather(bf16[32,8,256]{2,1,0:T(8,128)(2,1)S(1)} %collective-permute-done), channel_id=1, replica_groups=mesh['yh'=2,'xz'=32,'ylo'=4,'core'=2] {'core'}, dimensions={0}, use_global_device_ids=true | all-gather | bytes 393216 | tf_op jit(solution)/shard_map/all_gather | solution.py:117
  53.8 0.6 all-to-all-done
  54.4 0.0 copy-done.3
  54.4 0.0 copy-done.5
  54.4 0.0 copy-done.6
  54.4 0.0 copy-done
  54.4 0.0 copy-done.1
  54.4 0.0 copy-done.2
  54.4 0.0 copy-done.4
  54.4 2.9 %shard_map.100 = bf16[4,512,128]{2,1,0:T(8,128)(2,1)S(1)} custom-call(f32[256]{0:T(256)} %gains_hbm.1, bf16[4,512,128]{2,1,0:T(8,128)(2,1)S(1)} %bitcast.10, bf16[512,256]{1,0:T(8,128)(2,1)S(1)} %bitcast.12, bf16[512,512]{1,0:T(8,128)(2,1)S(1)} %copy-done, bf16[512,512]{1,0:T(8,128)(2,1)S(1)} %copy-done.1, bf16[256,256]{1,0:T(8,128)(2,1)S(1)} %copy-done.4, ...), custom_call_target="tpu_custom_call" | custom-call | tf_op jit(solution)/shard_map/pallas_call | solution.py:120
  57.3 34.9 %all_to_all.15 = bf16[256,8,128]{2,1,0:T(8,128)(2,1)S(1)} all-to-all(bf16[256,8,128]{2,1,0:T(8,128)(2,1)S(1)} %bitcast.11), channel_id=1, replica_groups={{4,12,20,28,36,44,52,60,68,76,84,92,100,108,116,124,132,140,148,156,164..., dimensions={0} | all-to-all | bytes 1048576 | tf_op jit(solution)/shard_map/all_to_all | solution.py:104
  92.2 1.1 %copy.16 = bf16[8,128,256]{2,1,0:T(8,128)(2,1)} copy(bf16[8,128,256]{1,0,2:T(8,128)(2,1)S(1)} %bitcast.13) | data formatting | bytes 1048576 | tf_op jit(solution)/shard_map/transpose | solution.py:130
Async XLA Ops:
  0.0 15.4 %copy-start.7 = (bf16[1,1024,256]{2,1,0:T(8,128)(2,1)S(1)}, bf16[1,1024,256]{2,1,0:T(8,128)(2,1)}, u32[]{:S(2)}) copy-start(bf16[1,1024,256]{2,1,0:T(8,128)(2,1)} %param.10) | copy-start | bytes 1572868
  1.7 22.9 %all-to-all-start.1 = ((bf16[32,8,256]{2,1,0:T(8,128)(2,1)}), bf16[32,8,256]{2,1,0:T(8,128)(2,1)S(1)}, u32[]{:S(2)}, u32[]{:S(2)}) async-start(bf16[32,8,256]{2,1,0:T(8,128)(2,1)} %copy.17), calls=%async_computation.1 | async-start | bytes 262144 | tf_op jit(solution)/shard_map/all_to_all | solution.py:112
  15.4 39.0 %copy-start.3 = (f32[512,128]{1,0:T(8,128)S(1)}, f32[512,128]{1,0:T(8,128)}, u32[]{:S(2)}) copy-start(f32[512,128]{1,0:T(8,128)} %constant.20.clone.sin_tw) | copy-start | bytes 786436
  15.4 39.0 %copy-start.5 = (bf16[256,256]{1,0:T(8,128)(2,1)S(1)}, bf16[256,256]{1,0:T(8,128)(2,1)}, u32[]{:S(2)}) copy-start(bf16[256,256]{1,0:T(8,128)(2,1)} %constant.18.clone.parity) | copy-start | bytes 393220
  15.4 39.0 %copy-start.6 = (bf16[128,128]{1,0:T(8,128)(2,1)S(1)}, bf16[128,128]{1,0:T(8,128)(2,1)}, u32[]{:S(2)}) copy-start(bf16[128,128]{1,0:T(8,128)(2,1)} %constant.17.clone.order) | copy-start | bytes 98308
  24.6 29.8 %copy-start = (bf16[512,512]{1,0:T(8,128)(2,1)S(1)}, bf16[512,512]{1,0:T(8,128)(2,1)}, u32[]{:S(2)}) copy-start(bf16[512,512]{1,0:T(8,128)(2,1)} %constant.14.clone.cos_rows) | copy-start | bytes 1572868
  24.6 29.9 %copy-start.1 = (bf16[512,512]{1,0:T(8,128)(2,1)S(1)}, bf16[512,512]{1,0:T(8,128)(2,1)}, u32[]{:S(2)}) copy-start(bf16[512,512]{1,0:T(8,128)(2,1)} %constant.15.clone.sin_rows) | copy-start | bytes 1572868
  24.6 29.8 %all-to-all-start = ((bf16[256,8,128]{2,1,0:T(8,128)(2,1)}), bf16[256,8,128]{2,1,0:T(8,128)(2,1)S(1)}, u32[]{:S(2)}, u32[]{:S(2)}) async-start(bf16[256,8,128]{2,1,0:T(8,128)(2,1)} %bitcast.1), calls=%async_computation | async-start | bytes 1048576 | tf_op jit(solution)/shard_map/all_to_all | solution.py:104
  37.6 16.8 %copy-start.2 = (f32[512,128]{1,0:T(8,128)S(1)}, f32[512,128]{1,0:T(8,128)}, u32[]{:S(2)}) copy-start(f32[512,128]{1,0:T(8,128)} %constant.19.clone.cos_tw) | copy-start | bytes 786436
  37.6 16.8 %copy-start.4 = (bf16[256,256]{1,0:T(8,128)(2,1)S(1)}, bf16[256,256]{1,0:T(8,128)(2,1)}, u32[]{:S(2)}) copy-start(bf16[256,256]{1,0:T(8,128)(2,1)} %constant.16.clone.inner) | copy-start | bytes 393220
  37.7 14.1 %collective-permute-start = (bf16[32,8,256]{2,1,0:T(8,128)(2,1)S(1)}, bf16[32,8,256]{2,1,0:T(8,128)(2,1)S(1)}, u32[]{:S(2)}, u32[]{:S(2)}) collective-permute-start(bf16[32,8,256]{2,1,0:T(8,128)(2,1)S(1)} %all-to-all-done.1), channel_id=1, source_target_pairs={{0,4},{1,260},{2,6},{3,262},{4,256},{5,0},{6,258},{7,2},{256,5},{2... | collective-permute-start | bytes 393224 | tf_op jit(solution)/shard_map/ppermute | solution.py:116
